TPU v7x, 256 devices: a whole 4x4x8 slice. The times are simulated.
256 devices in a mesh: gz: 8 (over z), xy: 32 (over x, y, core).
Axes of the slice: x: 4, y: 4, z: 8, core: 2. Of those that a mesh axis runs over, the one named last changes fastest.
Arguments:
- volume: float32 [128, 1536, 128], P('gz', 'xy'), may hold values from 0 to 1
- measured: float32 [2, 5, 160, 1536], P(None, None, 'gz', 'xy'), may hold values from 0 to 1
- view_order: int32 [48], replicated, may hold values from 0 to 47, each once
Outputs:
- volume_out: float32 [128, 1536, 128], P('gz', 'xy')
- residual: float32 [5, 160, 1536], P(None, 'gz', 'xy')
Inputs may be any that keep to these rules, and one draw needn't show every extreme that they name: `view_order`: A permutation of the numbers 0 to 47.
All inputs are finite; a program needn't handle non-finite values.
Results may differ from a plain program's by a relative error of at most 0.00078.
Values may be sent and summed in bfloat16 or wider, within the bound.
No kernel may reach another device: no remote copies, remote signals or barrier semaphores. Data moves between devices by JAX's collectives and lax.ppermute only.
A program may use at most 64 MiB of HBM per device.

v0:
```python
import functools
import math

import jax
import jax.numpy as jnp
from jax import lax
from jax.experimental import pallas as pl
from jax.experimental.pallas import tpu as pltpu
from jax.sharding import PartitionSpec as P

Z_DEV = 16
X_DEV = 48
NY = 128
COLS_DEV = 48
ROWS_DEV = 20
VIEWS = 5
SUBSETS = 2
ANGLES = 48
N_XY = 32
N_GZ = 8
NX = X_DEV * N_XY
NZ = Z_DEV * N_GZ
DR = ROWS_DEV * N_GZ
DC = COLS_DEV * N_XY

WIN = 176
LANES = 256
MEAS_AT = LANES - COLS_DEV
Z_HALO = 6
Z_ALL = Z_DEV + 2 * Z_HALO
ONES = Z_ALL
Z_PAD = 32
GROUPS = 6
ROWS_PER = (5, 4)
ROWS_BELOW = (3, 0)
M_HALO = 8
M_ROWS = 40
FULL = 15 * 128
SUMS = 4
TILE = 16
TILES_Y = NY // TILE
TILES = X_DEV // TILE * TILES_Y
VOXELS = TILE * TILE
COLS_TILE = 40
VOLUME = (Z_DEV, X_DEV, NY)
PLACE = (0, 40, 80, 128, 168)
DEPTH = 208
HALO_ROWS = Z_HALO * X_DEV
INNER_ROWS = HALO_ROWS // 2
EDGE_AT = HALO_ROWS + INNER_ROWS
EDGE_ROWS = SUBSETS * VIEWS * M_HALO
SENT_ROWS = EDGE_AT + EDGE_ROWS
PITCH = 56
OUT_PITCH = 24
TABLE = (16, 128)
SHIFT_AT = 32
TILE_AT = 64


def iota(shape, dim):
    return lax.broadcasted_iota(jnp.int32, shape, dim)


def slice_of(i, gz):
    low = Z_DEV * gz - Z_HALO + (i - Z_DEV)
    high = Z_DEV * gz + Z_DEV + (i - Z_DEV - Z_HALO)
    return jnp.where(i < Z_DEV, Z_DEV * gz + i, jnp.where(i < Z_DEV + Z_HALO, low, high))


def hat(row, z):
    position = (DR - 1) / 2.0 + 0.96 * (DR / NZ) * (z.astype(jnp.float32) - (NZ - 1) / 2.0)
    value = jnp.maximum(0.0, 1.0 - jnp.abs(position - row.astype(jnp.float32)) / 2.0)
    ok = (row >= 0) & (row < DR) & (z >= 0) & (z < NZ)
    return jnp.where(ok, value, 0.0)


def first_row(gz, subset):
    return ROWS_DEV * gz - ROWS_BELOW[subset] - ((gz + 1) >> 1)


def slot_weights(group, slot, i, gz, subset):
    per = ROWS_PER[subset]
    row = first_row(gz, subset) + group * per + slot
    return jnp.where((slot < per) & (i < Z_ALL), hat(row, slice_of(i, gz)), 0.0)


def tile_offsets(table_ref, subset, tile):
    return [
        pl.multiple_of(table_ref[subset * VIEWS + v, TILE_AT + tile], 8) for v in range(VIEWS)
    ]


def coordinate(x, y, cosine, sine):
    xc = x - (NX - 1) / 2.0
    yc = y - (NY - 1) / 2.0
    source = 2.0 * NX
    along = xc * cosine + yc * sine
    depth = yc * cosine - xc * sine
    return (DC - 1) / 2.0 + 0.9 * (DC / NX) * along * source / (source + depth)


def fill_table(cosine, sine, xy):
    lane = iota(TABLE, 1)
    tile = lane - TILE_AT
    is_tile = lane >= TILE_AT
    strip = lane & (N_XY - 1)
    x = jnp.where(is_tile, xy * X_DEV + (tile >> 3) * TILE, strip * X_DEV).astype(jnp.float32)
    y = jnp.where(is_tile, (tile & 7) * TILE, 0).astype(jnp.float32)
    dx = jnp.where(is_tile, TILE - 1.0, X_DEV - 1.0)
    dy = jnp.where(is_tile, TILE - 1.0, NY - 1.0)
    least = jnp.minimum(
        jnp.minimum(coordinate(x, y, cosine, sine), coordinate(x + dx, y, cosine, sine)),
        jnp.minimum(coordinate(x, y + dy, cosine, sine), coordinate(x + dx, y + dy, cosine, sine)),
    )
    least = jnp.floor(least).astype(jnp.int32)
    start = least - 2
    own = jnp.sum(jnp.where(lane == xy, start, 0).astype(jnp.float32), axis=1, keepdims=True)
    tiles = jnp.maximum(least - 1 - own.astype(jnp.int32), 0) & ~7
    table = jnp.where(lane < SHIFT_AT, start & ~127, start & 127)
    return jnp.where(is_tile, tiles, table), own


def positions(u_ref, cosine, sine, own, subset, xy):
    t = iota((TILES, VOXELS), 0)
    l = iota((TILES, VOXELS), 1)
    x = ((t >> 3) * TILE + (l >> 4) + xy * X_DEV).astype(jnp.float32)
    y = ((t & 7) * TILE + (l & 15)).astype(jnp.float32)
    for v in range(VIEWS):
        at = subset * VIEWS + v
        u = coordinate(x, y, cosine[at : at + 1, 0:1], sine[at : at + 1, 0:1])
        u_ref[v] = u - own[at : at + 1, :]


def weights(u_ref, offsets, tile):
    c = iota((COLS_TILE, VOXELS), 0).astype(jnp.float32)
    pieces = []
    for v in range(VIEWS):
        u = u_ref[v, pl.ds(tile, 1), :] - offsets[v].astype(jnp.float32)
        pieces.append(jnp.maximum(0.0, 1.0 - jnp.abs(u - c)))
    pieces.insert(3, jnp.zeros((8, VOXELS), jnp.float32))
    return jnp.concatenate(pieces, axis=0).astype(jnp.bfloat16)


def forward(w_ref, slices, acc_ref, m_ref, table_ref, out_ref, subset, gz):
    acc_ref[...] = jnp.zeros_like(acc_ref)
    for tile in range(TILES):
        offsets = tile_offsets(table_ref, subset, tile)
        part = lax.dot_general(
            w_ref[tile],
            jnp.concatenate([slices(tile)] * 4, axis=0),
            (((1,), (1,)), ((), ())),
            preferred_element_type=jnp.float32,
        )
        for v in range(VIEWS):
            acc_ref[v, pl.ds(offsets[v], COLS_TILE), :] += part[PLACE[v] : PLACE[v] + COLS_TILE]
    per = ROWS_PER[subset]
    half = per + 1
    size = GROUPS * 2 * half
    k = iota((size, 128), 0)
    lane = iota((size, 128), 1)
    i = lane & (Z_PAD - 1)
    group = (k * 43) >> 9 if half == 6 else (k * 205) >> 11
    slot = k - group * 2 * half
    is_low = slot < half
    slot = jnp.where(is_low, slot, slot - half)
    rows = slot_weights(group, slot, i, gz, subset)
    rows = jnp.where((slot == per) & (i == ONES), 1.0, rows)
    rounded = rows.astype(jnp.bfloat16).astype(jnp.float32)
    rows = jnp.where(lane < 2 * Z_PAD, rounded, rows - rounded).astype(jnp.bfloat16)
    left_over = (iota((WIN, 128), 1) & Z_PAD) != 0
    used = GROUPS * VIEWS * 2 * half
    out_ref[used:, :] = jnp.zeros((out_ref.shape[0] - used, 128), jnp.float32)
    for v in range(VIEWS):
        sums = acc_ref[v]
        rounded = sums.astype(jnp.bfloat16).astype(jnp.float32)
        sums = jnp.where(left_over, sums - rounded, rounded).astype(jnp.bfloat16)
        sums = lax.dot_general(
            rows, sums, (((1,), (1,)), ((), ())), preferred_element_type=jnp.float32
        )
        high = jnp.concatenate(
            (sums[:, 128:WIN], jnp.zeros((size, LANES - WIN), jnp.float32)), axis=1
        )
        part = jnp.where(is_low, sums[:, 0:128], high) + m_ref[v, 0:size, :]
        out_ref[v * size : (v + 1) * size, :] = part


def smear(recv_ref, sm_ref, gz):
    i = iota((Z_PAD, GROUPS * 8), 0)
    k = iota((Z_PAD, GROUPS * 8), 1)
    rows = slot_weights(k >> 3, k & 7, i, gz, 0)
    ones = iota((Z_PAD, LANES), 0) == ONES
    for v in range(VIEWS):
        got = recv_ref[v * GROUPS : (v + 1) * GROUPS]
        got = got.astype(jnp.float32).reshape(GROUPS * 8, LANES)
        smeared = jnp.dot(
            rows, got, precision=lax.Precision.HIGHEST, preferred_element_type=jnp.float32
        )
        sm_ref[v] = jnp.where(ones, 1.0, smeared).astype(jnp.bfloat16).astype(jnp.float32)


def smear_last(recv_ref, sm_ref, res_ref, gz):
    size = 2 * Z_PAD + 24
    i = iota((size, GROUPS * 8), 0)
    k = iota((size, GROUPS * 8), 1)
    part = k & 7
    rows = slot_weights(k >> 3, part & 3, i & (Z_PAD - 1), gz, 1)
    rows = jnp.where((part >= 4) == (i >= Z_PAD), rows, 0.0)
    j = i - 2 * Z_PAD + ((gz + 1) >> 1)
    picked = (k == ((j >> 2) << 3) + 4 + (j & 3)).astype(jnp.float32)
    rows = jnp.where(i >= 2 * Z_PAD, picked, rows)
    ones = iota((Z_PAD, LANES), 0) == ONES
    part = iota((GROUPS * 8, 128), 0) & 7
    exact = (part >= 4) & (iota((GROUPS * 8, 128), 1) >= MEAS_AT - 128)
    for v in range(VIEWS):
        got = recv_ref[v * GROUPS * 8 : (v + 1) * GROUPS * 8, :]
        got = jnp.where(exact, got, got.astype(jnp.bfloat16).astype(jnp.float32))
        sums = jnp.dot(
            rows, got, precision=lax.Precision.HIGHEST, preferred_element_type=jnp.float32
        )
        smeared = jnp.concatenate((sums[0:Z_PAD], sums[Z_PAD : 2 * Z_PAD]), axis=1)
        sm_ref[v] = jnp.where(ones, 1.0, smeared).astype(jnp.bfloat16).astype(jnp.float32)
        own = pltpu.roll(sums[2 * Z_PAD :], 256 - MEAS_AT, 1)
        res_ref[v] = own[0:ROWS_DEV, 0:COLS_DEV]


def windows(sm_ref, offsets):
    lane = iota((Z_PAD, 128), 1)
    placed = []
    for v in range(VIEWS):
        at = PLACE[v] & 127
        shift = (at - offsets[v]) & 127
        low = pltpu.roll(sm_ref[v, :, 0:128], shift, 1)
        high = pltpu.roll(sm_ref[v, :, 128:256], shift, 1)
        placed.append(jnp.where(lane < at + 128 - offsets[v], low, high))
    first = jnp.where(lane < 40, placed[0], jnp.where(lane < 80, placed[1], placed[2]))
    first = jnp.where(lane < 120, first, 0.0)
    second = jnp.where(lane < 40, placed[3], jnp.where(lane < 80, placed[4], 0.0))
    both = jnp.concatenate((first, second), axis=1)
    return both.astype(jnp.bfloat16)[:, 0:DEPTH]


def backward(w_ref, sm_ref, table_ref, old, store, subset, gz):
    zi = slice_of(iota((Z_PAD, LANES), 0), gz)
    inside = iota((Z_PAD, LANES), 0) < Z_ALL
    total = jnp.sum(jnp.where(inside, hat(iota((Z_PAD, LANES), 1), zi), 0.0), axis=1, keepdims=True)

    for tile in range(TILES):
        offsets = tile_offsets(table_ref, subset, tile)
        back = jnp.dot(
            windows(sm_ref, offsets), w_ref[tile], preferred_element_type=jnp.float32
        )
        norm = total * back[ONES : ONES + 1, :]
        store(tile, old(tile), back / jnp.maximum(norm, 1.0))


def swap_blocks(rows):
    block = iota((8, 128), 1) >> 4
    for d in (4, 2, 1):
        high = (block & d) != 0
        new = list(rows)
        for i in range(8):
            if i & d == 0:
                a, b = (rows[i], rows[i + d])
                new[i] = jnp.where(high, pltpu.roll(b, 16 * d, 1), a)
                new[i + d] = jnp.where(high, b, pltpu.roll(a, 128 - 16 * d, 1))
        rows = new
    return rows


def relay(source_ref, out_ref, pitch):
    def step(xb, nothing):
        for half in range(2):
            for b in range(2):
                at = xb * TILE + half * 8 + b * 8 * pitch
                rows = [source_ref[pl.ds(at + i, 8, stride=pitch), :] for i in range(8)]
                for q, block in enumerate(swap_blocks(rows)):
                    out_ref[
                        xb * TILES_Y + q, b * 8 : b * 8 + 8, half * 128 : half * 128 + 128
                    ] = block
        return nothing

    lax.fori_loop(0, X_DEV // TILE, step, 0)


def pack_kernel(vol_ref, meas_ref, up_ref, down_ref, row_ref):
    row_ref[...] = jnp.zeros_like(row_ref)
    for out_ref, z, inner, r in (
        (up_ref, Z_DEV - Z_HALO, Z_HALO // 2, ROWS_DEV - M_HALO),
        (down_ref, 0, 0, 0),
    ):
        slices = vol_ref[z * X_DEV : (z + Z_HALO) * X_DEV, :]
        rounded = slices.astype(jnp.bfloat16)
        out_ref[0:HALO_ROWS, :] = rounded
        left = slices - rounded.astype(jnp.float32)
        at = inner * X_DEV
        out_ref[HALO_ROWS:EDGE_AT, :] = left[at : at + INNER_ROWS].astype(jnp.bfloat16)
        for v in range(VIEWS):
            at = (v * ROWS_DEV + r) * SUBSETS
            row_ref[:, 0:COLS_DEV] = meas_ref[at : at + SUBSETS * M_HALO, :]
            row = row_ref[...]
            rounded = row.astype(jnp.bfloat16).astype(jnp.float32)
            both = pltpu.roll(rounded, MEAS_AT - 128, 1)
            both = both + pltpu.roll(row - rounded, MEAS_AT - 128 - COLS_DEV, 1)
            at = EDGE_AT + v * SUBSETS * M_HALO
            out_ref[at : at + SUBSETS * M_HALO, :] = both.astype(jnp.bfloat16)


def prepare_kernel(
    cosine_ref, sine_ref, vol_ref, meas_ref,
    w0_ref, w1_ref, own_ref, mown_ref, flat_ref, table_ref, sem, u_ref,
):
    xy = lax.axis_index("xy")
    cosine = cosine_ref[...]
    sine = sine_ref[...]
    flat_ref[...], own = fill_table(cosine, sine, xy)
    copy = pltpu.make_async_copy(flat_ref, table_ref, sem)
    copy.start()
    relay(vol_ref, own_ref, X_DEV)
    mown_ref[...] = jnp.zeros_like(mown_ref)
    for s in range(SUBSETS):
        for v in range(VIEWS):
            for at, count in ((0, 8), (8, 8), (16, 4)):
                rows = meas_ref[pl.ds((v * ROWS_DEV + at) * 2 + s, count, stride=2), :]
                mown_ref[s, v, at : at + count, MEAS_AT - 128 : 128] = rows
    copy.wait()
    for subset, w_ref in ((0, w0_ref), (1, w1_ref)):
        positions(u_ref, cosine, sine, own, subset, xy)

        def step(tt, nothing):
            for t in range(8):
                tile = tt * 8 + t
                w_ref[tile] = weights(u_ref, tile_offsets(table_ref, subset, tile), tile)
            return nothing

        lax.fori_loop(0, TILES // 8, step, 0)


def first_kernel(
    flat_ref, w_ref, own_ref, mown_ref, low_ref, high_ref,
    out_ref, side_ref, m1_ref, table_ref, sem, halo_ref, acc_ref, raw_ref, m0_ref, edge_ref,
):
    gz = lax.axis_index("gz")
    copy = pltpu.make_async_copy(flat_ref, table_ref, sem)
    copy.start()
    for side, (sent_ref, inner) in enumerate(((low_ref, Z_HALO // 2), (high_ref, 0))):
        left_at = HALO_ROWS - inner * X_DEV
        for z in range(Z_HALO):
            at = z * X_DEV
            rows = sent_ref[at : at + X_DEV, :].astype(jnp.float32)
            if inner <= z < inner + Z_HALO // 2:
                rows = rows + sent_ref[left_at + at : left_at + at + X_DEV, :].astype(jnp.float32)
            at = (side * Z_HALO + z) * PITCH
            halo_ref[at : at + X_DEV, :] = rows
        edge = sent_ref[EDGE_AT:SENT_ROWS, :].astype(jnp.float32)
        edge = edge + pltpu.roll(edge, COLS_DEV, 1)
        edge_ref[side] = jnp.where(iota(edge.shape, 1) >= MEAS_AT - 128, edge, 0.0)
    for z in range(2 * Z_HALO, Z_DEV):
        value = 1.0 if z == ONES - Z_DEV else 0.0
        halo_ref[z * PITCH : z * PITCH + X_DEV, :] = jnp.full((X_DEV, NY), value, jnp.float32)
    relay(halo_ref, side_ref, PITCH)
    for s, m_ref in ((0, m0_ref), (1, m1_ref)):
        per = ROWS_PER[s]
        m_ref[...] = jnp.zeros_like(m_ref)
        for v in range(VIEWS):
            edge = pl.ds(v * 2 * M_HALO + s, M_HALO, stride=2)
            high = edge_ref[1, edge, :]
            joined = jnp.concatenate(
                (
                    edge_ref[0, edge, :],
                    mown_ref[s, v, 0:16, :],
                    jnp.concatenate((mown_ref[s, v, 16:20, :], high[0:4]), axis=0),
                    jnp.concatenate((high[4:8], jnp.zeros((4, 128), jnp.float32)), axis=0),
                ),
                axis=0,
            )
            raw_ref[s, v] = pltpu.roll(
                joined, M_ROWS + ((gz + 1) >> 1) - (M_HALO - ROWS_BELOW[s]), 0
            )
            for group in range(GROUPS):
                at = group * 2 * (per + 1) + per + 1
                m_ref[v, at : at + per, :] = raw_ref[s, v, group * per : (group + 1) * per, :]

    def slices(tile):
        return jnp.concatenate((own_ref[tile], side_ref[tile]), axis=0).astype(jnp.bfloat16)

    copy.wait()
    forward(w_ref, slices, acc_ref, m0_ref, table_ref, out_ref, 0, gz)


def middle_kernel(
    flat_ref, recv_ref, own_ref, side_ref, m_ref, w0_ref, w1_ref,
    out_ref, new_ref, table_ref, sem, sm_ref, vb_ref, acc_ref,
):
    gz = lax.axis_index("gz")
    copy = pltpu.make_async_copy(flat_ref, table_ref, sem)
    copy.start()
    smear(recv_ref, sm_ref, gz)
    copy.wait()
    ones = iota((Z_PAD, VOXELS), 0) == ONES

    def old(tile):
        return jnp.concatenate((own_ref[tile], side_ref[tile]), axis=0)

    def store(tile, old, change):
        new = jnp.where(ones, 1.0, old + change)
        new_ref[tile] = new[0:Z_DEV]
        vb_ref[tile] = new.astype(jnp.bfloat16)

    backward(w0_ref, sm_ref, table_ref, old, store, 0, gz)
    forward(w1_ref, lambda tile: vb_ref[tile], acc_ref, m_ref, table_ref, out_ref, 1, gz)


def last_kernel(
    flat_ref, recv_ref, old_ref, w_ref,
    out_ref, res_ref, table_ref, sem, sm_ref, new_ref, block_ref, sems,
):
    gz = lax.axis_index("gz")
    copy = pltpu.make_async_copy(flat_ref, table_ref, sem)
    copy.start()
    smear_last(recv_ref, sm_ref, res_ref, gz)
    copy.wait()
    copies = []

    def store(tile, old, change):
        new_ref[tile] = old + change[0:Z_DEV]
        xb = tile // TILES_Y
        if tile % TILES_Y < TILES_Y - 1:
            return
        for half in range(2):
            for b in range(Z_DEV // 8):
                blocks = [
                    new_ref[xb * TILES_Y + q, b * 8 : b * 8 + 8, half * 128 : half * 128 + 128]
                    for q in range(TILES_Y)
                ]
                at = half * 8 + b * 8 * OUT_PITCH
                for i, row in enumerate(swap_blocks(blocks)):
                    block_ref[xb, pl.ds(at + i, 8, stride=OUT_PITCH), :] = row
        for z in range(Z_DEV):
            copies.append(
                pltpu.make_async_copy(
                    block_ref.at[xb, pl.ds(z * OUT_PITCH, TILE), :],
                    out_ref.at[z, pl.ds(xb * TILE, TILE), :],
                    sems.at[xb, z],
                )
            )
            copies[-1].start()

    backward(w_ref, sm_ref, table_ref, lambda tile: old_ref[tile], store, 1, gz)
    for copy in copies:
        copy.wait()


def owner_kernel(flat_ref, recv_ref, out_ref, table_ref, sem, acc_ref, sum_ref, mea_ref, *, subset):
    gz = lax.axis_index("gz")
    xy = lax.axis_index("xy")
    copy = pltpu.make_async_copy(flat_ref, table_ref, sem)
    copy.start()
    view = jnp.minimum(xy // GROUPS, VIEWS - 1)
    group = xy % GROUPS
    at = subset * VIEWS + view
    per = ROWS_PER[subset]
    half = per + 1
    lane = iota((8, 128), 1)
    sum_ref[...] = jnp.zeros_like(sum_ref)
    mea_ref[...] = jnp.zeros_like(mea_ref)
    end = N_XY * 2 * half - 8

    def upper(s):
        row = s * 2 * half + half
        last = recv_ref[min(row, end) : min(row, end) + 8, :]
        return pltpu.roll(last, 8 - (row - end), 0) if row > end else last

    for s in range(N_XY):
        column = s * COLS_DEV
        own = jnp.where(lane >= MEAS_AT - 128, upper(s), 0.0)
        own = pltpu.roll(own, (column + 256 - MEAS_AT) % 128, 1)
        block = column // 128 * 128
        offset = column - block
        mea_ref[:, block : block + 128] += jnp.where(lane >= offset, own, 0.0)
        if offset + COLS_DEV > 128:
            mea_ref[:, block + 128 : block + 256] += jnp.where(lane < offset, own, 0.0)
    copy.wait()
    for s in range(N_XY):
        base = pl.multiple_of(table_ref[at, s], 128)
        shift = table_ref[at, SHIFT_AT + s]
        row = s * 2 * half
        low = pltpu.roll(recv_ref[row : row + 8, :], shift, 1)
        high = pltpu.roll(jnp.where(lane < WIN - 128, upper(s), 0.0), shift, 1)
        wrapped = lane < shift
        part_ref = sum_ref.at[s % SUMS]
        part_ref[:, pl.ds(base, 128)] += jnp.where(wrapped, 0.0, low)
        part_ref[:, pl.ds(base + 128, 128)] += jnp.where(wrapped, low, high)
        part_ref[:, pl.ds(base + 256, 128)] += jnp.where(wrapped, high, 0.0)
    slot = iota((8, NZ), 0)
    row = first_row(gz, subset) + group * per + slot
    ray_rows = jnp.where(slot < per, hat(row, iota((8, NZ), 1)), 0.0)
    ray_rows = jnp.sum(ray_rows, axis=1, keepdims=True)
    sums = sum_ref[0]
    for part in range(1, SUMS):
        sums = sums + sum_ref[part]
    totals = sums[per : per + 1, :]
    acc_ref[...] = mea_ref[...] - sums / jnp.maximum(ray_rows * totals, 1.0)
    for t in range(N_XY):
        base = pl.multiple_of(table_ref[at, t], 128)
        shift = table_ref[at, SHIFT_AT + t]
        back = (128 - shift) & 127
        a = pltpu.roll(acc_ref[:, pl.ds(base, 128)], back, 1)
        b = pltpu.roll(acc_ref[:, pl.ds(base + 128, 128)], back, 1)
        c = pltpu.roll(acc_ref[:, pl.ds(base + 256, 128)], back, 1)
        kept = lane < 128 - shift
        low = jnp.where(kept, a, b)
        high = jnp.where(kept, b, c)
        if subset == 0:
            out_ref[t, :, 0:128] = low.astype(jnp.bfloat16)
            out_ref[t, :, 128:256] = high.astype(jnp.bfloat16)
            continue
        column = t * COLS_DEV
        block = column // 128 * 128
        offset = column - block
        turn = (MEAS_AT - 128 - offset) % 128
        own = pltpu.roll(acc_ref[:, block : block + 128], turn, 1)
        if offset + COLS_DEV > 128:
            more = pltpu.roll(acc_ref[:, block + 128 : block + 256], turn, 1)
            own = jnp.where(lane < MEAS_AT - offset, own, more)
        high = jnp.where(lane >= MEAS_AT - 128, own, high)
        out_ref[t * 8 : (t + 1) * 8, :] = jnp.where(slot < 4, low, pltpu.roll(high, 4, 0))


def call(kernel, inputs, outs, scratch, name, table=True):
    vmem = pl.BlockSpec(memory_space=pltpu.VMEM)
    anywhere = pl.BlockSpec(memory_space=pl.ANY)
    inputs = [pltpu.with_memory_space_constraint(x, pltpu.VMEM) for x in inputs]
    if table:
        scratch = [pltpu.SMEM(TABLE, jnp.int32), pltpu.SemaphoreType.DMA, *scratch]
    return pl.pallas_call(
        kernel,
        in_specs=[vmem] * len(inputs),
        out_specs=[anywhere if out.shape == VOLUME else vmem for out in outs],
        out_shape=outs,
        scratch_shapes=scratch,
        compiler_params=pltpu.CompilerParams(vmem_limit_bytes=12 * 1024 * 1024),
        name=name,
    )(*inputs)


def exchanged(parts, shape):
    sent = lax.all_to_all(
        parts.reshape(shape), "xy", split_axis=0, concat_axis=0, tiled=True
    )
    return sent.reshape(parts.shape)


def local(volume, measured, view_order):
    f32 = jnp.float32
    bf16 = jnp.bfloat16
    vmem = pltpu.VMEM
    angles = 2.0 * math.pi * view_order[: SUBSETS * VIEWS].astype(f32) / ANGLES
    angles = jnp.broadcast_to(jnp.pad(angles, (0, TABLE[0] - SUBSETS * VIEWS))[:, None], TABLE)
    flat = pltpu.with_memory_space_constraint(volume.reshape(Z_DEV * X_DEV, NY), vmem)
    rows = measured.transpose(1, 2, 0, 3).reshape(VIEWS * ROWS_DEV * SUBSETS, COLS_DEV)
    made = vmem((TILES, DEPTH, VOXELS), bf16)
    slices = vmem((TILES, Z_DEV, VOXELS), f32)
    sm_scratch = vmem((VIEWS, Z_PAD, LANES), f32)
    acc_scratch = vmem((VIEWS, WIN, 128), f32)
    row_scratch = vmem((8, FULL), f32)
    owner_scratch = [row_scratch, vmem((SUMS, 8, FULL), f32), row_scratch]

    sent = vmem((SENT_ROWS, 128), bf16)
    up, down = call(
        pack_kernel,
        (flat, rows),
        [sent, sent],
        [vmem((SUBSETS * M_HALO, 128), f32)],
        "pack",
        table=False,
    )
    next_up = [(i, (i + 1) % N_GZ) for i in range(N_GZ)]
    low = lax.ppermute(up, "gz", next_up)
    high = lax.ppermute(down, "gz", [(j, i) for i, j in next_up])
    w0, w1, own, mown, table = call(
        prepare_kernel,
        (jnp.cos(angles), jnp.sin(angles), flat, rows),
        [made, made, slices, vmem((SUBSETS, VIEWS, 24, 128), f32), vmem(TABLE, jnp.int32)],
        [vmem((VIEWS, TILES, VOXELS), f32)],
        "prepare",
    )
    partial, side, m1 = call(
        first_kernel,
        (table, w0, own, mown, low, high),
        [vmem((N_XY * 12, 128), f32), slices, vmem((VIEWS, 64, 128), f32)],
        [
            vmem((Z_DEV * PITCH, NY), f32),
            acc_scratch,
            vmem((SUBSETS, VIEWS, M_ROWS, 128), f32),
            vmem((VIEWS, 72, 128), f32),
            vmem((2, EDGE_ROWS, 128), f32),
        ],
        "first",
    )
    (rounded,) = call(
        functools.partial(owner_kernel, subset=0),
        (table, exchanged(partial, (N_XY, 3, 4, 128))),
        [vmem((N_XY, 8, LANES), bf16)],
        owner_scratch,
        "owner_a",
    )
    partial, new = call(
        middle_kernel,
        (table, exchanged(rounded, rounded.shape), own, side, m1, w0, w1),
        [vmem((N_XY * 10, 128), f32), slices],
        [sm_scratch, vmem((TILES, Z_PAD, VOXELS), bf16), acc_scratch],
        "middle",
    )
    (final,) = call(
        functools.partial(owner_kernel, subset=1),
        (table, exchanged(partial, (N_XY, 5, 2, 128))),
        [vmem((N_XY * 8, 128), f32)],
        owner_scratch,
        "owner_b",
    )
    volume_out, residual = call(
        last_kernel,
        (table, exchanged(final, (N_XY, 8, 128)), new, w1),
        [
            jax.ShapeDtypeStruct(VOLUME, f32),
            jax.ShapeDtypeStruct((VIEWS, ROWS_DEV, COLS_DEV), f32),
        ],
        [
            sm_scratch,
            slices,
            vmem((X_DEV // TILE, Z_DEV * OUT_PITCH, NY), f32),
            pltpu.SemaphoreType.DMA((X_DEV // TILE, Z_DEV)),
        ],
        "last",
    )
    return volume_out, residual


def solution(mesh):
    in_specs = (P("gz", "xy", None), P(None, None, "gz", "xy"), P())
    out_specs = (P("gz", "xy", None), P(None, "gz", "xy"))
    return jax.shard_map(local, mesh=mesh, in_specs=in_specs, out_specs=out_specs, check_vma=False)
```

profile of v0, /device:TPU:1, one launch (start us, length us, event | category | flops | bytes accessed | tf_op | source)
XLA Modules:
  0.0 76.8 jit_solution(10843608417541773329)
XLA Ops:
  0.6 0.0 copy-start
  0.6 1.0 %copy-done = f32[16,48,128]{2,1,0:T(8,128)S(1)} copy-done((f32[16,48,128]{2,1,0:T(8,128)S(1)}, f32[16,48,128]{2,1,0:T(8,128)}, u32[]{:S(2)}) %copy-start) | copy-done | bytes 393240
  1.6 0.0 copy-start.2
  1.6 0.9 %copy-done.2 = f32[2,5,20,48]{3,0,2,1:T(2,128)S(1)} copy-done((f32[2,5,20,48]{3,0,2,1:T(2,128)S(1)}, f32[2,5,20,48]{3,0,2,1:T(2,128)}, u32[]{:S(2)}) %copy-start.2) | copy-done | bytes 38424
  2.5 0.1 pack.1
  2.7 2.5 %collective-permute-start = (bf16[512,128]{1,0:T(8,128)(2,1)S(1)}, bf16[512,128]{1,0:T(8,128)(2,1)S(1)}, u32[]{:S(2)}, u32[]{:S(2)}) collective-permute-start(bf16[512,128]{1,0:T(8,128)(2,1)S(1)} %get-tuple-element.18), channel_id=1, source_target_pairs={{0,32},{32,64},{64,96},{96,128},{128,160},{160,192},{192,224},{224... | collective-permute-start | bytes 393224 | tf_op jit(solution)/shard_map/ppermute | solution.py:578
  5.2 4.0 %collective-permute-start.1 = (bf16[512,128]{1,0:T(8,128)(2,1)S(1)}, bf16[512,128]{1,0:T(8,128)(2,1)S(1)}, u32[]{:S(2)}, u32[]{:S(2)}) collective-permute-start(bf16[512,128]{1,0:T(8,128)(2,1)S(1)} %get-tuple-element.19), channel_id=1, source_target_pairs={{32,0},{64,32},{96,64},{128,96},{160,128},{192,160},{224,192},{0,2... | collective-permute-start | bytes 393224 | tf_op jit(solution)/shard_map/ppermute | solution.py:579
  9.2 0.7 convert_multiply_fusion
  9.9 0.1 broadcast_in_dim.9.sine_ref
  10.0 0.1 broadcast_in_dim.8.cosine_ref
  10.1 0.0 copy-start.1
  10.1 1.0 %copy-done.1 = f32[16,48,128]{2,1,0:T(8,128)S(1)} copy-done((f32[16,48,128]{2,1,0:T(8,128)S(1)}, f32[16,48,128]{2,1,0:T(8,128)}, u32[]{:S(2)}) %copy-start.1) | copy-done | bytes 393240
  11.1 0.0 copy-start.3
  11.1 0.9 %copy-done.3 = f32[2,5,20,48]{3,0,2,1:T(2,128)S(1)} copy-done((f32[2,5,20,48]{3,0,2,1:T(2,128)S(1)}, f32[2,5,20,48]{3,0,2,1:T(2,128)}, u32[]{:S(2)}) %copy-start.3) | copy-done | bytes 38424
  12.0 2.8 %prepare.1 = (bf16[24,208,256]{2,1,0:T(8,128)(2,1)S(1)}, bf16[24,208,256]{2,1,0:T(8,128)(2,1)S(1)}, f32[24,16,256]{2,1,0:T(8,128)S(1)}, f32[2,5,24,128]{3,2,1,0:T(8,128)S(1)}, s32[16,128]{1,0:T(8,128)S(1)}) custom-call(f32[16,128]{1,0:T(8,128)S(1)} %broadcast_in_dim.8.cosine_ref, f32[16,128]{1,0:T(8,128)S(1)} %broadcast_in_dim.9.sine_ref, ...), custom_call_target="tpu_custom_call" | custom-call | tf_op jit(solution)/shard_map/prepare/pallas_call | solution.py:535
  14.7 0.0 collective-permute-done.low_ref
  14.7 0.0 collective-permute-done.1.high_ref
  14.8 2.1 %first.1 = (f32[384,128]{1,0:T(8,128)S(1)}, f32[24,16,256]{2,1,0:T(8,128)S(1)}, f32[5,64,128]{2,1,0:T(8,128)S(1)}) custom-call(s32[16,128]{1,0:T(8,128)S(1)} %get-tuple-element.14.flat_ref, bf16[24,208,256]{2,1,0:T(8,128)(2,1)S(1)} %get-tuple-element.15.w_ref.w0_ref, f32[24,16,256]{2,1,0:T(8,128)S(1)} %get-tuple-element.16.own_ref, ...), custom_call_target="tpu_custom_call" | custom-call | tf_op jit(solution)/shard_map/first/pallas_call | solution.py:535
  16.9 16.1 %all_to_all.20 = f32[32,3,4,128]{3,2,1,0:T(4,128)S(1)} all-to-all(f32[32,3,4,128]{3,2,1,0:T(4,128)S(1)} %bitcast.18), channel_id=1, replica_groups=mesh['gz'=8,'xy'=32] {'xy'}, dimensions={0} | all-to-all | bytes 393216 | tf_op jit(solution)/shard_map/all_to_all | solution.py:547
  33.0 1.4 %owner_a.1 = bf16[32,8,256]{2,1,0:T(8,128)(2,1)S(1)} custom-call(s32[16,128]{1,0:T(8,128)S(1)} %get-tuple-element.14.flat_ref, f32[384,128]{1,0:T(8,128)S(1)} %bitcast.12), custom_call_target="tpu_custom_call" | custom-call | tf_op jit(solution)/shard_map/owner_a/pallas_call | solution.py:535
  34.5 11.2 %all_to_all.21.recv_ref = bf16[32,8,256]{2,1,0:T(8,128)(2,1)S(1)} all-to-all(bf16[32,8,256]{2,1,0:T(8,128)(2,1)S(1)} %owner_a.1), channel_id=1, replica_groups=mesh['gz'=8,'xy'=32] {'xy'}, dimensions={0} | all-to-all | bytes 262144 | tf_op jit(solution)/shard_map/all_to_all | solution.py:547
  45.7 2.5 %middle.1 = (f32[320,128]{1,0:T(8,128)S(1)}, f32[24,16,256]{2,1,0:T(8,128)S(1)}) custom-call(s32[16,128]{1,0:T(8,128)S(1)} %get-tuple-element.14.flat_ref, bf16[32,8,256]{2,1,0:T(8,128)(2,1)S(1)} %all_to_all.21.recv_ref, f32[24,16,256]{2,1,0:T(8,128)S(1)} %get-tuple-element.16.own_ref, f32[24,16,256]{2,1,0:T(8,128)S(1)} %get-tuple-element.21.side_ref, ...), custom_call_target="tpu_custom_call" | custom-call | tf_op jit(solution)/shard_map/middle/pallas_call | solution.py:535
  48.2 11.5 %all_to_all.22 = f32[32,5,2,128]{3,2,1,0:T(2,128)S(1)} all-to-all(f32[32,5,2,128]{3,2,1,0:T(2,128)S(1)} %bitcast.19), channel_id=1, replica_groups=mesh['gz'=8,'xy'=32] {'xy'}, dimensions={0} | all-to-all | bytes 327680 | tf_op jit(solution)/shard_map/all_to_all | solution.py:547
  59.8 1.5 %owner_b.1 = f32[256,128]{1,0:T(8,128)S(1)} custom-call(s32[16,128]{1,0:T(8,128)S(1)} %get-tuple-element.14.flat_ref, f32[320,128]{1,0:T(8,128)S(1)} %bitcast.13), custom_call_target="tpu_custom_call" | custom-call | tf_op jit(solution)/shard_map/owner_b/pallas_call | solution.py:535
  61.2 11.2 %all_to_all.23 = f32[32,8,128]{2,1,0:T(8,128)S(1)} all-to-all(f32[32,8,128]{2,1,0:T(8,128)S(1)} %bitcast.15), channel_id=1, replica_groups=mesh['gz'=8,'xy'=32] {'xy'}, dimensions={0} | all-to-all | bytes 262144 | tf_op jit(solution)/shard_map/all_to_all | solution.py:547
  72.5 4.4 %last.1 = (f32[16,48,128]{2,1,0:T(8,128)}, f32[5,20,48]{2,1,0:T(8,128)}) custom-call(s32[16,128]{1,0:T(8,128)S(1)} %get-tuple-element.14.flat_ref, f32[256,128]{1,0:T(8,128)S(1)} %bitcast.14, f32[24,16,256]{2,1,0:T(8,128)S(1)} %get-tuple-element.25.old_ref, bf16[24,208,256]{2,1,0:T(8,128)(2,1)S(1)} %get-tuple-element.23.w1_ref.w_ref), custom_call_target="tpu_custom_call" | custom-call | tf_op jit(solution)/shard_map/last/pallas_call | solution.py:535
  (1 shorter events, 0.0 us)
Async XLA Ops:
  0.6 1.0 %copy-start = (f32[16,48,128]{2,1,0:T(8,128)S(1)}, f32[16,48,128]{2,1,0:T(8,128)}, u32[]{:S(2)}) copy-start(f32[16,48,128]{2,1,0:T(8,128)} %param.3) | copy-start | bytes 1179652
  1.6 0.9 %copy-start.2 = (f32[2,5,20,48]{3,0,2,1:T(2,128)S(1)}, f32[2,5,20,48]{3,0,2,1:T(2,128)}, u32[]{:S(2)}) copy-start(f32[2,5,20,48]{3,0,2,1:T(2,128)} %param.4) | copy-start | bytes 115204
  2.7 12.1 %collective-permute-start = (bf16[512,128]{1,0:T(8,128)(2,1)S(1)}, bf16[512,128]{1,0:T(8,128)(2,1)S(1)}, u32[]{:S(2)}, u32[]{:S(2)}) collective-permute-start(bf16[512,128]{1,0:T(8,128)(2,1)S(1)} %get-tuple-element.18), channel_id=1, source_target_pairs={{0,32},{32,64},{64,96},{96,128},{128,160},{160,192},{192,224},{224... | collective-permute-start | bytes 393224 | tf_op jit(solution)/shard_map/ppermute | solution.py:578
  5.2 9.6 %collective-permute-start.1 = (bf16[512,128]{1,0:T(8,128)(2,1)S(1)}, bf16[512,128]{1,0:T(8,128)(2,1)S(1)}, u32[]{:S(2)}, u32[]{:S(2)}) collective-permute-start(bf16[512,128]{1,0:T(8,128)(2,1)S(1)} %get-tuple-element.19), channel_id=1, source_target_pairs={{32,0},{64,32},{96,64},{128,96},{160,128},{192,160},{224,192},{0,2... | collective-permute-start | bytes 393224 | tf_op jit(solution)/shard_map/ppermute | solution.py:579
  10.1 1.0 %copy-start.1 = (f32[16,48,128]{2,1,0:T(8,128)S(1)}, f32[16,48,128]{2,1,0:T(8,128)}, u32[]{:S(2)}) copy-start(f32[16,48,128]{2,1,0:T(8,128)} %param.3) | copy-start | bytes 1179652
  11.1 0.9 %copy-start.3 = (f32[2,5,20,48]{3,0,2,1:T(2,128)S(1)}, f32[2,5,20,48]{3,0,2,1:T(2,128)}, u32[]{:S(2)}) copy-start(f32[2,5,20,48]{3,0,2,1:T(2,128)} %param.4) | copy-start | bytes 115204
where the time goes:
time: 77.2 us; the launch traced here: 76.8 us
  blocking collectives  50.1 us (65%)
  Pallas kernels  14.8 us (19%)
  starting transfers between devices  6.56 us (8%)
  local copies, waits for them, and re-layouts  3.97 us (5%)
    all_to_all x4, blocking collectives, exchanged(): lax.all_to_all(parts.reshape(shape), 'xy', split_axis=0, concat_axis=0, t...  50.1 us
    pallas_call x7, Pallas kernels, call(): pl.pallas_call(kernel, in_specs=[vmem] * len(inputs), out_specs=[anywhere...  14.8 us
    ppermute x1, starting transfers between devices, local(): high = lax.ppermute(down, 'gz', [(j, i) for i, j in next_up])  4.03 us
    unnamed x8, local copies, waits for them, and re-layouts  3.78 us
    ppermute x1, starting transfers between devices, local(): low = lax.ppermute(up, 'gz', next_up)  2.53 us
  transfers between devices with their start and end apart: 2, of which 0 were waited for; matrix products, arithmetic and copies ran while one was open for 1% of the time, Pallas kernels for 4%

commit v1 on v0

--- a/solution.py
+++ b/solution.py
@@ -282,8 +282,18 @@
     lax.fori_loop(0, X_DEV // TILE, step, 0)
 
 
-def pack_kernel(vol_ref, meas_ref, up_ref, down_ref, row_ref):
+def pack_kernel(
+    vol_hbm, meas_hbm, up_ref, down_ref, vol_ref, meas_ref, row_ref, sems
+):
+    copies = [
+        pltpu.make_async_copy(vol_hbm, vol_ref, sems.at[0]),
+        pltpu.make_async_copy(meas_hbm, meas_ref, sems.at[1]),
+    ]
+    for copy in copies:
+        copy.start()
     row_ref[...] = jnp.zeros_like(row_ref)
+    for copy in copies:
+        copy.wait()
     for out_ref, z, inner, r in (
         (up_ref, Z_DEV - Z_HALO, Z_HALO // 2, ROWS_DEV - M_HALO),
         (down_ref, 0, 0, 0),
@@ -419,13 +429,13 @@
     copy.start()
     smear_last(recv_ref, sm_ref, res_ref, gz)
     copy.wait()
-    copies = []
 
     def store(tile, old, change):
         new_ref[tile] = old + change[0:Z_DEV]
-        xb = tile // TILES_Y
-        if tile % TILES_Y < TILES_Y - 1:
-            return
+
+    backward(w_ref, sm_ref, table_ref, lambda tile: old_ref[tile], store, 1, gz)
+    copies = []
+    for xb in range(X_DEV // TILE):
         for half in range(2):
             for b in range(Z_DEV // 8):
                 blocks = [
@@ -435,17 +445,14 @@
                 at = half * 8 + b * 8 * OUT_PITCH
                 for i, row in enumerate(swap_blocks(blocks)):
                     block_ref[xb, pl.ds(at + i, 8, stride=OUT_PITCH), :] = row
-        for z in range(Z_DEV):
-            copies.append(
-                pltpu.make_async_copy(
-                    block_ref.at[xb, pl.ds(z * OUT_PITCH, TILE), :],
-                    out_ref.at[z, pl.ds(xb * TILE, TILE), :],
-                    sems.at[xb, z],
-                )
+        copies.append(
+            pltpu.make_async_copy(
+                block_ref.at[xb].reshape(Z_DEV, OUT_PITCH, NY).at[:, 0:TILE, :],
+                out_ref.at[:, pl.ds(xb * TILE, TILE), :],
+                sems.at[xb],
             )
-            copies[-1].start()
-
-    backward(w_ref, sm_ref, table_ref, lambda tile: old_ref[tile], store, 1, gz)
+        )
+        copies[-1].start()
     for copy in copies:
         copy.wait()
 
@@ -526,12 +533,11 @@
         out_ref[t * 8 : (t + 1) * 8, :] = jnp.where(slot < 4, low, pltpu.roll(high, 4, 0))
 
 
-def call(kernel, inputs, outs, scratch, name, table=True):
+def call(kernel, inputs, outs, scratch, name):
     vmem = pl.BlockSpec(memory_space=pltpu.VMEM)
     anywhere = pl.BlockSpec(memory_space=pl.ANY)
     inputs = [pltpu.with_memory_space_constraint(x, pltpu.VMEM) for x in inputs]
-    if table:
-        scratch = [pltpu.SMEM(TABLE, jnp.int32), pltpu.SemaphoreType.DMA, *scratch]
+    scratch = [pltpu.SMEM(TABLE, jnp.int32), pltpu.SemaphoreType.DMA, *scratch]
     return pl.pallas_call(
         kernel,
         in_specs=[vmem] * len(inputs),
@@ -556,7 +562,7 @@
     vmem = pltpu.VMEM
     angles = 2.0 * math.pi * view_order[: SUBSETS * VIEWS].astype(f32) / ANGLES
     angles = jnp.broadcast_to(jnp.pad(angles, (0, TABLE[0] - SUBSETS * VIEWS))[:, None], TABLE)
-    flat = pltpu.with_memory_space_constraint(volume.reshape(Z_DEV * X_DEV, NY), vmem)
+    flat = volume.reshape(Z_DEV * X_DEV, NY)
     rows = measured.transpose(1, 2, 0, 3).reshape(VIEWS * ROWS_DEV * SUBSETS, COLS_DEV)
     made = vmem((TILES, DEPTH, VOXELS), bf16)
     slices = vmem((TILES, Z_DEV, VOXELS), f32)
@@ -566,14 +572,15 @@
     owner_scratch = [row_scratch, vmem((SUMS, 8, FULL), f32), row_scratch]
 
     sent = vmem((SENT_ROWS, 128), bf16)
-    up, down = call(
+    up, down, flat, rows = pl.pallas_call(
         pack_kernel,
-        (flat, rows),
-        [sent, sent],
-        [vmem((SUBSETS * M_HALO, 128), f32)],
-        "pack",
-        table=False,
-    )
+        in_specs=[pl.BlockSpec(memory_space=pl.ANY)] * 2,
+        out_specs=[pl.BlockSpec(memory_space=vmem)] * 4,
+        out_shape=[sent, sent, vmem(flat.shape, f32), vmem(rows.shape, f32)],
+        scratch_shapes=[vmem((SUBSETS * M_HALO, 128), f32), pltpu.SemaphoreType.DMA((2,))],
+        compiler_params=pltpu.CompilerParams(vmem_limit_bytes=12 * 1024 * 1024),
+        name="pack",
+    )(flat, rows)
     next_up = [(i, (i + 1) % N_GZ) for i in range(N_GZ)]
     low = lax.ppermute(up, "gz", next_up)
     high = lax.ppermute(down, "gz", [(j, i) for i, j in next_up])
@@ -629,7 +636,7 @@
             sm_scratch,
             slices,
             vmem((X_DEV // TILE, Z_DEV * OUT_PITCH, NY), f32),
-            pltpu.SemaphoreType.DMA((X_DEV // TILE, Z_DEV)),
+            pltpu.SemaphoreType.DMA((X_DEV // TILE,)),
         ],
         "last",
     )

time: 77.2 us -> 75.2 us (0.974)
  local copies, waits for them, and re-layouts: 3.97 us -> 2.07 us
    unnamed x8 -> x4, local copies, waits for them, and re-layouts: 3.78 us -> 1.88 us
    pallas_call x7 -> x6, Pallas kernels: 14.8 us -> 14.3 us  [call(): pl.pallas_call(kernel, in_specs=[vmem] * len(inputs), out_specs=[anywhere...]
where the time goes in v1:
time: 75.2 us; the launch traced here: 74.9 us
  blocking collectives  50.1 us (67%)
  Pallas kernels  14.8 us (20%)
  starting transfers between devices  6.56 us (9%)
  local copies, waits for them, and re-layouts  2.07 us (3%)
    all_to_all x4, blocking collectives, exchanged(): lax.all_to_all(parts.reshape(shape), 'xy', split_axis=0, concat_axis=0, t...  50.1 us
    pallas_call x6, Pallas kernels, call(): pl.pallas_call(kernel, in_specs=[vmem] * len(inputs), out_specs=[anywhere...  14.3 us
    ppermute x1, starting transfers between devices, local(): high = lax.ppermute(down, 'gz', [(j, i) for i, j in next_up])  4.03 us
    ppermute x1, starting transfers between devices, local(): low = lax.ppermute(up, 'gz', next_up)  2.53 us
    unnamed x4, local copies, waits for them, and re-layouts  1.88 us
  transfers between devices with their start and end apart: 2, of which 0 were waited for; matrix products, arithmetic and copies ran while one was open for 1% of the time, Pallas kernels for 4%

profile of v1, /device:TPU:1, one launch (start us, length us, event | category | flops | bytes accessed | tf_op | source)
XLA Modules:
  0.0 74.9 jit_solution(4208038880133661407)
XLA Ops:
  0.6 0.0 copy-start
  0.6 1.0 %copy-done = f32[16,48,128]{2,1,0:T(8,128)S(1)} copy-done((f32[16,48,128]{2,1,0:T(8,128)S(1)}, f32[16,48,128]{2,1,0:T(8,128)}, u32[]{:S(2)}) %copy-start) | copy-done | bytes 393240
  1.6 0.0 copy-start.1
  1.6 0.9 %copy-done.1 = f32[2,5,20,48]{3,0,2,1:T(2,128)S(1)} copy-done((f32[2,5,20,48]{3,0,2,1:T(2,128)S(1)}, f32[2,5,20,48]{3,0,2,1:T(2,128)}, u32[]{:S(2)}) %copy-start.1) | copy-done | bytes 38424
  2.5 0.5 pack.1
  3.0 2.5 %collective-permute-start = (bf16[512,128]{1,0:T(8,128)(2,1)S(1)}, bf16[512,128]{1,0:T(8,128)(2,1)S(1)}, u32[]{:S(2)}, u32[]{:S(2)}) collective-permute-start(bf16[512,128]{1,0:T(8,128)(2,1)S(1)} %get-tuple-element.22), channel_id=1, source_target_pairs={{0,32},{32,64},{64,96},{96,128},{128,160},{160,192},{192,224},{224... | collective-permute-start | bytes 393224 | tf_op jit(solution)/shard_map/ppermute | solution.py:585
  5.5 4.0 %collective-permute-start.1 = (bf16[512,128]{1,0:T(8,128)(2,1)S(1)}, bf16[512,128]{1,0:T(8,128)(2,1)S(1)}, u32[]{:S(2)}, u32[]{:S(2)}) collective-permute-start(bf16[512,128]{1,0:T(8,128)(2,1)S(1)} %get-tuple-element.23), channel_id=1, source_target_pairs={{32,0},{64,32},{96,64},{128,96},{160,128},{192,160},{224,192},{0,2... | collective-permute-start | bytes 393224 | tf_op jit(solution)/shard_map/ppermute | solution.py:586
  9.6 0.7 convert_multiply_fusion
  10.3 0.1 broadcast_in_dim.9.sine_ref
  10.4 0.1 broadcast_in_dim.8.cosine_ref
  10.4 2.8 %prepare.1 = (bf16[24,208,256]{2,1,0:T(8,128)(2,1)S(1)}, bf16[24,208,256]{2,1,0:T(8,128)(2,1)S(1)}, f32[24,16,256]{2,1,0:T(8,128)S(1)}, f32[2,5,24,128]{3,2,1,0:T(8,128)S(1)}, s32[16,128]{1,0:T(8,128)S(1)}) custom-call(f32[16,128]{1,0:T(8,128)S(1)} %broadcast_in_dim.8.cosine_ref, f32[16,128]{1,0:T(8,128)S(1)} %broadcast_in_dim.9.sine_ref, ...), custom_call_target="tpu_custom_call" | custom-call | tf_op jit(solution)/shard_map/prepare/pallas_call | solution.py:541
  13.2 0.0 collective-permute-done.low_ref
  13.2 0.0 collective-permute-done.1.high_ref
  13.2 2.1 %first.1 = (f32[384,128]{1,0:T(8,128)S(1)}, f32[24,16,256]{2,1,0:T(8,128)S(1)}, f32[5,64,128]{2,1,0:T(8,128)S(1)}) custom-call(s32[16,128]{1,0:T(8,128)S(1)} %get-tuple-element.18.flat_ref, bf16[24,208,256]{2,1,0:T(8,128)(2,1)S(1)} %get-tuple-element.19.w_ref.w0_ref, f32[24,16,256]{2,1,0:T(8,128)S(1)} %get-tuple-element.20.own_ref, ...), custom_call_target="tpu_custom_call" | custom-call | tf_op jit(solution)/shard_map/first/pallas_call | solution.py:541
  15.4 16.1 %all_to_all.20 = f32[32,3,4,128]{3,2,1,0:T(4,128)S(1)} all-to-all(f32[32,3,4,128]{3,2,1,0:T(4,128)S(1)} %bitcast.15), channel_id=1, replica_groups=mesh['gz'=8,'xy'=32] {'xy'}, dimensions={0} | all-to-all | bytes 393216 | tf_op jit(solution)/shard_map/all_to_all | solution.py:553
  31.5 1.4 %owner_a.1 = bf16[32,8,256]{2,1,0:T(8,128)(2,1)S(1)} custom-call(s32[16,128]{1,0:T(8,128)S(1)} %get-tuple-element.18.flat_ref, f32[384,128]{1,0:T(8,128)S(1)} %bitcast.10), custom_call_target="tpu_custom_call" | custom-call | tf_op jit(solution)/shard_map/owner_a/pallas_call | solution.py:541
  33.0 11.2 %all_to_all.21.recv_ref = bf16[32,8,256]{2,1,0:T(8,128)(2,1)S(1)} all-to-all(bf16[32,8,256]{2,1,0:T(8,128)(2,1)S(1)} %owner_a.1), channel_id=1, replica_groups=mesh['gz'=8,'xy'=32] {'xy'}, dimensions={0} | all-to-all | bytes 262144 | tf_op jit(solution)/shard_map/all_to_all | solution.py:553
  44.2 2.5 %middle.1 = (f32[320,128]{1,0:T(8,128)S(1)}, f32[24,16,256]{2,1,0:T(8,128)S(1)}) custom-call(s32[16,128]{1,0:T(8,128)S(1)} %get-tuple-element.18.flat_ref, bf16[32,8,256]{2,1,0:T(8,128)(2,1)S(1)} %all_to_all.21.recv_ref, f32[24,16,256]{2,1,0:T(8,128)S(1)} %get-tuple-element.20.own_ref, f32[24,16,256]{2,1,0:T(8,128)S(1)} %get-tuple-element.25.side_ref, ...), custom_call_target="tpu_custom_call" | custom-call | tf_op jit(solution)/shard_map/middle/pallas_call | solution.py:541
  46.7 11.5 %all_to_all.22 = f32[32,5,2,128]{3,2,1,0:T(2,128)S(1)} all-to-all(f32[32,5,2,128]{3,2,1,0:T(2,128)S(1)} %bitcast.16), channel_id=1, replica_groups=mesh['gz'=8,'xy'=32] {'xy'}, dimensions={0} | all-to-all | bytes 327680 | tf_op jit(solution)/shard_map/all_to_all | solution.py:553
  58.2 1.5 %owner_b.1 = f32[256,128]{1,0:T(8,128)S(1)} custom-call(s32[16,128]{1,0:T(8,128)S(1)} %get-tuple-element.18.flat_ref, f32[320,128]{1,0:T(8,128)S(1)} %bitcast.11), custom_call_target="tpu_custom_call" | custom-call | tf_op jit(solution)/shard_map/owner_b/pallas_call | solution.py:541
  59.7 11.2 %all_to_all.23 = f32[32,8,128]{2,1,0:T(8,128)S(1)} all-to-all(f32[32,8,128]{2,1,0:T(8,128)S(1)} %bitcast.13), channel_id=1, replica_groups=mesh['gz'=8,'xy'=32] {'xy'}, dimensions={0} | all-to-all | bytes 262144 | tf_op jit(solution)/shard_map/all_to_all | solution.py:553
  70.9 4.0 %last.1 = (f32[16,48,128]{2,1,0:T(8,128)}, f32[5,20,48]{2,1,0:T(8,128)}) custom-call(s32[16,128]{1,0:T(8,128)S(1)} %get-tuple-element.18.flat_ref, f32[256,128]{1,0:T(8,128)S(1)} %bitcast.12, f32[24,16,256]{2,1,0:T(8,128)S(1)} %get-tuple-element.29.old_ref, bf16[24,208,256]{2,1,0:T(8,128)(2,1)S(1)} %get-tuple-element.27.w1_ref.w_ref), custom_call_target="tpu_custom_call" | custom-call | tf_op jit(solution)/shard_map/last/pallas_call | solution.py:541
  (1 shorter events, 0.0 us)
Async XLA Ops:
  0.6 1.0 %copy-start = (f32[16,48,128]{2,1,0:T(8,128)S(1)}, f32[16,48,128]{2,1,0:T(8,128)}, u32[]{:S(2)}) copy-start(f32[16,48,128]{2,1,0:T(8,128)} %param.3) | copy-start | bytes 1179652
  1.6 0.9 %copy-start.1 = (f32[2,5,20,48]{3,0,2,1:T(2,128)S(1)}, f32[2,5,20,48]{3,0,2,1:T(2,128)}, u32[]{:S(2)}) copy-start(f32[2,5,20,48]{3,0,2,1:T(2,128)} %param.4) | copy-start | bytes 115204
  3.0 10.2 %collective-permute-start = (bf16[512,128]{1,0:T(8,128)(2,1)S(1)}, bf16[512,128]{1,0:T(8,128)(2,1)S(1)}, u32[]{:S(2)}, u32[]{:S(2)}) collective-permute-start(bf16[512,128]{1,0:T(8,128)(2,1)S(1)} %get-tuple-element.22), channel_id=1, source_target_pairs={{0,32},{32,64},{64,96},{96,128},{128,160},{160,192},{192,224},{224... | collective-permute-start | bytes 393224 | tf_op jit(solution)/shard_map/ppermute | solution.py:585
  5.5 7.7 %collective-permute-start.1 = (bf16[512,128]{1,0:T(8,128)(2,1)S(1)}, bf16[512,128]{1,0:T(8,128)(2,1)S(1)}, u32[]{:S(2)}, u32[]{:S(2)}) collective-permute-start(bf16[512,128]{1,0:T(8,128)(2,1)S(1)} %get-tuple-element.23), channel_id=1, source_target_pairs={{32,0},{64,32},{96,64},{128,96},{160,128},{192,160},{224,192},{0,2... | collective-permute-start | bytes 393224 | tf_op jit(solution)/shard_map/ppermute | solution.py:586

commit v2 on v1

--- a/solution.py
+++ b/solution.py
@@ -185,16 +185,22 @@
 
 
 def smear(recv_ref, sm_ref, gz):
-    i = iota((Z_PAD, GROUPS * 8), 0)
-    k = iota((Z_PAD, GROUPS * 8), 1)
-    rows = slot_weights(k >> 3, k & 7, i, gz, 0)
+    i = iota((3 * Z_PAD, GROUPS * 8), 0)
+    k = iota((3 * Z_PAD, GROUPS * 8), 1)
+    part = k & 7
+    third = i >> 5
+    slot = jnp.where(third == 0, part, 2 * (part - 5) + third - 1)
+    rows = slot_weights(k >> 3, slot, i & (Z_PAD - 1), gz, 0)
+    rows = jnp.where((third == 0) == (part < 5), rows, 0.0)
     ones = iota((Z_PAD, LANES), 0) == ONES
     for v in range(VIEWS):
         got = recv_ref[v * GROUPS : (v + 1) * GROUPS]
-        got = got.astype(jnp.float32).reshape(GROUPS * 8, LANES)
-        smeared = jnp.dot(
+        got = got.astype(jnp.float32).reshape(GROUPS * 8, 128)
+        sums = jnp.dot(
             rows, got, precision=lax.Precision.HIGHEST, preferred_element_type=jnp.float32
         )
+        high = sums[Z_PAD : 2 * Z_PAD] + pltpu.roll(sums[2 * Z_PAD :], 128 - COLS_DEV, 1)
+        smeared = jnp.concatenate((sums[0:Z_PAD], high), axis=1)
         sm_ref[v] = jnp.where(ones, 1.0, smeared).astype(jnp.bfloat16).astype(jnp.float32)
 
 
@@ -283,11 +289,12 @@
 
 
 def pack_kernel(
-    vol_hbm, meas_hbm, up_ref, down_ref, vol_ref, meas_ref, row_ref, sems
+    vol_hbm, meas_hbm, order_hbm, up_ref, down_ref, vol_ref, meas_ref, order_ref, row_ref, sems
 ):
     copies = [
         pltpu.make_async_copy(vol_hbm, vol_ref, sems.at[0]),
         pltpu.make_async_copy(meas_hbm, meas_ref, sems.at[1]),
+        pltpu.make_async_copy(order_hbm, order_ref, sems.at[2]),
     ]
     for copy in copies:
         copy.start()
@@ -316,12 +323,16 @@
 
 
 def prepare_kernel(
-    cosine_ref, sine_ref, vol_ref, meas_ref,
-    w0_ref, w1_ref, own_ref, mown_ref, flat_ref, table_ref, sem, u_ref,
+    order_ref, vol_ref, meas_ref,
+    w0_ref, w1_ref, own_ref, mown_ref, table_ref, u_ref, flat_ref, sem,
 ):
     xy = lax.axis_index("xy")
-    cosine = cosine_ref[...]
-    sine = sine_ref[...]
+    chosen = iota((TABLE[0], ANGLES), 0) == iota((TABLE[0], ANGLES), 1)
+    chosen = jnp.where(chosen, order_ref[...].astype(jnp.float32), 0.0)
+    chosen = jnp.broadcast_to(jnp.sum(chosen, axis=1, keepdims=True), TABLE)
+    angles = 2.0 * math.pi * chosen / ANGLES
+    cosine = jnp.cos(angles)
+    sine = jnp.sin(angles)
     flat_ref[...], own = fill_table(cosine, sine, xy)
     copy = pltpu.make_async_copy(flat_ref, table_ref, sem)
     copy.start()
@@ -346,12 +357,10 @@
 
 
 def first_kernel(
-    flat_ref, w_ref, own_ref, mown_ref, low_ref, high_ref,
-    out_ref, side_ref, m1_ref, table_ref, sem, halo_ref, acc_ref, raw_ref, m0_ref, edge_ref,
+    table_ref, w_ref, own_ref, mown_ref, low_ref, high_ref,
+    out_ref, side_ref, m1_ref, halo_ref, acc_ref, raw_ref, m0_ref, edge_ref,
 ):
     gz = lax.axis_index("gz")
-    copy = pltpu.make_async_copy(flat_ref, table_ref, sem)
-    copy.start()
     for side, (sent_ref, inner) in enumerate(((low_ref, Z_HALO // 2), (high_ref, 0))):
         left_at = HALO_ROWS - inner * X_DEV
         for z in range(Z_HALO):
@@ -393,19 +402,15 @@
     def slices(tile):
         return jnp.concatenate((own_ref[tile], side_ref[tile]), axis=0).astype(jnp.bfloat16)
 
-    copy.wait()
     forward(w_ref, slices, acc_ref, m0_ref, table_ref, out_ref, 0, gz)
 
 
 def middle_kernel(
-    flat_ref, recv_ref, own_ref, side_ref, m_ref, w0_ref, w1_ref,
-    out_ref, new_ref, table_ref, sem, sm_ref, vb_ref, acc_ref,
+    table_ref, recv_ref, own_ref, side_ref, m_ref, w0_ref, w1_ref,
+    out_ref, new_ref, sm_ref, vb_ref, acc_ref,
 ):
     gz = lax.axis_index("gz")
-    copy = pltpu.make_async_copy(flat_ref, table_ref, sem)
-    copy.start()
     smear(recv_ref, sm_ref, gz)
-    copy.wait()
     ones = iota((Z_PAD, VOXELS), 0) == ONES
 
     def old(tile):
@@ -421,20 +426,18 @@
 
 
 def last_kernel(
-    flat_ref, recv_ref, old_ref, w_ref,
-    out_ref, res_ref, table_ref, sem, sm_ref, new_ref, block_ref, sems,
+    table_ref, recv_ref, old_ref, w_ref,
+    out_ref, res_ref, sm_ref, new_ref, block_ref, own_ref, sems,
 ):
     gz = lax.axis_index("gz")
-    copy = pltpu.make_async_copy(flat_ref, table_ref, sem)
-    copy.start()
-    smear_last(recv_ref, sm_ref, res_ref, gz)
-    copy.wait()
+    smear_last(recv_ref, sm_ref, own_ref, gz)
+    copies = [pltpu.make_async_copy(own_ref, res_ref, sems.at[X_DEV // TILE])]
+    copies[0].start()
 
     def store(tile, old, change):
         new_ref[tile] = old + change[0:Z_DEV]
 
     backward(w_ref, sm_ref, table_ref, lambda tile: old_ref[tile], store, 1, gz)
-    copies = []
     for xb in range(X_DEV // TILE):
         for half in range(2):
             for b in range(Z_DEV // 8):
@@ -457,11 +460,9 @@
         copy.wait()
 
 
-def owner_kernel(flat_ref, recv_ref, out_ref, table_ref, sem, acc_ref, sum_ref, mea_ref, *, subset):
+def owner_kernel(table_ref, recv_ref, out_ref, acc_ref, sum_ref, mea_ref, *, subset):
     gz = lax.axis_index("gz")
     xy = lax.axis_index("xy")
-    copy = pltpu.make_async_copy(flat_ref, table_ref, sem)
-    copy.start()
     view = jnp.minimum(xy // GROUPS, VIEWS - 1)
     group = xy % GROUPS
     at = subset * VIEWS + view
@@ -486,7 +487,6 @@
         mea_ref[:, block : block + 128] += jnp.where(lane >= offset, own, 0.0)
         if offset + COLS_DEV > 128:
             mea_ref[:, block + 128 : block + 256] += jnp.where(lane < offset, own, 0.0)
-    copy.wait()
     for s in range(N_XY):
         base = pl.multiple_of(table_ref[at, s], 128)
         shift = table_ref[at, SHIFT_AT + s]
@@ -518,8 +518,15 @@
         low = jnp.where(kept, a, b)
         high = jnp.where(kept, b, c)
         if subset == 0:
-            out_ref[t, :, 0:128] = low.astype(jnp.bfloat16)
-            out_ref[t, :, 128:256] = high.astype(jnp.bfloat16)
+            other = pltpu.roll(high, COLS_DEV, 1)
+            even = jnp.where(
+                slot == 5,
+                pltpu.roll(high, 5, 0),
+                jnp.where(slot == 6, pltpu.roll(high, 4, 0), pltpu.roll(high, 3, 0)),
+            )
+            odd = jnp.where(slot == 5, pltpu.roll(other, 4, 0), pltpu.roll(other, 3, 0))
+            rest = jnp.where(lane < COLS_DEV, even, odd)
+            out_ref[t] = jnp.where(slot < 5, low, rest).astype(jnp.bfloat16)
             continue
         column = t * COLS_DEV
         block = column // 128 * 128
@@ -535,13 +542,22 @@
 
 def call(kernel, inputs, outs, scratch, name):
     vmem = pl.BlockSpec(memory_space=pltpu.VMEM)
+    smem = pl.BlockSpec(memory_space=pltpu.SMEM)
     anywhere = pl.BlockSpec(memory_space=pl.ANY)
-    inputs = [pltpu.with_memory_space_constraint(x, pltpu.VMEM) for x in inputs]
-    scratch = [pltpu.SMEM(TABLE, jnp.int32), pltpu.SemaphoreType.DMA, *scratch]
+
+    def spec(x):
+        if x.dtype == jnp.int32:
+            return smem
+        return anywhere if isinstance(x, jax.ShapeDtypeStruct) else vmem
+
+    inputs = [
+        x if x.dtype == jnp.int32 else pltpu.with_memory_space_constraint(x, pltpu.VMEM)
+        for x in inputs
+    ]
     return pl.pallas_call(
         kernel,
-        in_specs=[vmem] * len(inputs),
-        out_specs=[anywhere if out.shape == VOLUME else vmem for out in outs],
+        in_specs=[spec(x) for x in inputs],
+        out_specs=[spec(x) for x in outs],
         out_shape=outs,
         scratch_shapes=scratch,
         compiler_params=pltpu.CompilerParams(vmem_limit_bytes=12 * 1024 * 1024),
@@ -560,9 +576,8 @@
     f32 = jnp.float32
     bf16 = jnp.bfloat16
     vmem = pltpu.VMEM
-    angles = 2.0 * math.pi * view_order[: SUBSETS * VIEWS].astype(f32) / ANGLES
-    angles = jnp.broadcast_to(jnp.pad(angles, (0, TABLE[0] - SUBSETS * VIEWS))[:, None], TABLE)
     flat = volume.reshape(Z_DEV * X_DEV, NY)
+    order = view_order.reshape(1, ANGLES)
     rows = measured.transpose(1, 2, 0, 3).reshape(VIEWS * ROWS_DEV * SUBSETS, COLS_DEV)
     made = vmem((TILES, DEPTH, VOXELS), bf16)
     slices = vmem((TILES, Z_DEV, VOXELS), f32)
@@ -572,25 +587,34 @@
     owner_scratch = [row_scratch, vmem((SUMS, 8, FULL), f32), row_scratch]
 
     sent = vmem((SENT_ROWS, 128), bf16)
-    up, down, flat, rows = pl.pallas_call(
+    hbm = pl.BlockSpec(memory_space=pltpu.HBM)
+    up, down, flat, rows, order = pl.pallas_call(
         pack_kernel,
-        in_specs=[pl.BlockSpec(memory_space=pl.ANY)] * 2,
-        out_specs=[pl.BlockSpec(memory_space=vmem)] * 4,
-        out_shape=[sent, sent, vmem(flat.shape, f32), vmem(rows.shape, f32)],
-        scratch_shapes=[vmem((SUBSETS * M_HALO, 128), f32), pltpu.SemaphoreType.DMA((2,))],
+        in_specs=[hbm] * 3,
+        out_specs=[pl.BlockSpec(memory_space=vmem)] * 5,
+        out_shape=[
+            sent, sent, vmem(flat.shape, f32), vmem(rows.shape, f32), vmem((1, ANGLES), jnp.int32)
+        ],
+        scratch_shapes=[vmem((SUBSETS * M_HALO, 128), f32), pltpu.SemaphoreType.DMA((3,))],
         compiler_params=pltpu.CompilerParams(vmem_limit_bytes=12 * 1024 * 1024),
         name="pack",
-    )(flat, rows)
+    )(*(pltpu.with_memory_space_constraint(x, pltpu.HBM) for x in (flat, rows, order)))
     next_up = [(i, (i + 1) % N_GZ) for i in range(N_GZ)]
     low = lax.ppermute(up, "gz", next_up)
     high = lax.ppermute(down, "gz", [(j, i) for i, j in next_up])
-    w0, w1, own, mown, table = call(
+    w0, w1, own, mown, table = pl.pallas_call(
         prepare_kernel,
-        (jnp.cos(angles), jnp.sin(angles), flat, rows),
-        [made, made, slices, vmem((SUBSETS, VIEWS, 24, 128), f32), vmem(TABLE, jnp.int32)],
-        [vmem((VIEWS, TILES, VOXELS), f32)],
-        "prepare",
-    )
+        in_specs=[pl.BlockSpec(memory_space=vmem)] * 3,
+        out_specs=[pl.BlockSpec(memory_space=m) for m in (vmem, vmem, vmem, vmem, pltpu.SMEM)],
+        out_shape=[
+            made, made, slices, vmem((SUBSETS, VIEWS, 24, 128), f32), pltpu.SMEM(TABLE, jnp.int32)
+        ],
+        scratch_shapes=[
+            vmem((VIEWS, TILES, VOXELS), f32), vmem(TABLE, jnp.int32), pltpu.SemaphoreType.DMA
+        ],
+        compiler_params=pltpu.CompilerParams(vmem_limit_bytes=12 * 1024 * 1024),
+        name="prepare",
+    )(*(pltpu.with_memory_space_constraint(x, vmem) for x in (order, flat, rows)))
     partial, side, m1 = call(
         first_kernel,
         (table, w0, own, mown, low, high),
@@ -607,7 +631,7 @@
     (rounded,) = call(
         functools.partial(owner_kernel, subset=0),
         (table, exchanged(partial, (N_XY, 3, 4, 128))),
-        [vmem((N_XY, 8, LANES), bf16)],
+        [vmem((N_XY, 8, 128), bf16)],
         owner_scratch,
         "owner_a",
     )
@@ -636,7 +660,8 @@
             sm_scratch,
             slices,
             vmem((X_DEV // TILE, Z_DEV * OUT_PITCH, NY), f32),
-            pltpu.SemaphoreType.DMA((X_DEV // TILE,)),
+            vmem((VIEWS, ROWS_DEV, COLS_DEV), f32),
+            pltpu.SemaphoreType.DMA((X_DEV // TILE + 1,)),
         ],
         "last",
     )

time: 75.2 us -> 70.1 us (0.932)
  Pallas kernels: 14.8 us -> 12.3 us
  local copies, waits for them, and re-layouts: 2.07 us -> 0 us
    pallas_call x7, Pallas kernels: 14.8 us -> 12.3 us  [the longest x5 8.28 us: call(): pl.pallas_call(kernel, in_specs=[spec(x) for x in inputs], out_specs=[spe...]
    unnamed x4 -> x0, local copies, waits for them, and re-layouts: 1.88 us -> none
  transfers between devices with their start and end apart: 2 -> 2, of which waited for: 0 -> 1; matrix products, arithmetic and copies ran while one was open for 1% -> 0% of each run, Pallas kernels for 4% -> 4%
where the time goes in v2:
time: 70.1 us; the launch traced here: 69.9 us
  blocking collectives  50.1 us (71%)
  Pallas kernels  12.3 us (18%)
  starting transfers between devices  6.56 us (9%)
    all_to_all x4, blocking collectives, exchanged(): lax.all_to_all(parts.reshape(shape), 'xy', split_axis=0, concat_axis=0, t...  50.1 us
    pallas_call x5, Pallas kernels, call(): pl.pallas_call(kernel, in_specs=[spec(x) for x in inputs], out_specs=[spe...  8.28 us
    ppermute x1, starting transfers between devices, local(): high = lax.ppermute(down, 'gz', [(j, i) for i, j in next_up])  4.03 us
    pallas_call x1, Pallas kernels, local(): pl.pallas_call(prepare_kernel, in_specs=[pl.BlockSpec(memory_space=vmem)]...  2.83 us
    ppermute x1, starting transfers between devices, local(): low = lax.ppermute(up, 'gz', next_up)  2.53 us
  transfers between devices with their start and end apart: 2, of which 1 were waited for; matrix products, arithmetic and copies ran while one was open for 0% of the time, Pallas kernels for 4%

profile of v2, /device:TPU:1, one launch (start us, length us, event | category | flops | bytes accessed | tf_op | source)
XLA Modules:
  0.0 69.9 jit_solution(16152571547983019570)
XLA Ops:
  0.6 1.2 %pack.1 = (bf16[512,128]{1,0:T(8,128)(2,1)S(1)}, bf16[512,128]{1,0:T(8,128)(2,1)S(1)}, f32[768,128]{1,0:T(8,128)S(1)}, f32[200,48]{1,0:T(8,128)S(1)}, s32[1,48]{1,0:T(1,128)S(1)}) custom-call(f32[768,128]{1,0:T(8,128)} %bitcast.17, f32[200,48]{1,0:T(8,128)} %bitcast.18, s32[1,48]{1,0:T(1,128)} %bitcast.19), custom_call_target="tpu_custom_call" | custom-call | tf_op jit(solution)/shard_map/pack/pallas_call | solution.py:591
  1.8 2.5 %collective-permute-start = (bf16[512,128]{1,0:T(8,128)(2,1)S(1)}, bf16[512,128]{1,0:T(8,128)(2,1)S(1)}, u32[]{:S(2)}, u32[]{:S(2)}) collective-permute-start(bf16[512,128]{1,0:T(8,128)(2,1)S(1)} %get-tuple-element.24), channel_id=1, source_target_pairs={{0,32},{32,64},{64,96},{96,128},{128,160},{160,192},{192,224},{224... | collective-permute-start | bytes 393224 | tf_op jit(solution)/shard_map/ppermute | solution.py:603
  4.4 4.0 %collective-permute-start.1 = (bf16[512,128]{1,0:T(8,128)(2,1)S(1)}, bf16[512,128]{1,0:T(8,128)(2,1)S(1)}, u32[]{:S(2)}, u32[]{:S(2)}) collective-permute-start(bf16[512,128]{1,0:T(8,128)(2,1)S(1)} %get-tuple-element.25), channel_id=1, source_target_pairs={{32,0},{64,32},{96,64},{128,96},{160,128},{192,160},{224,192},{0,2... | collective-permute-start | bytes 393224 | tf_op jit(solution)/shard_map/ppermute | solution.py:604
  8.4 2.8 %prepare.1 = (bf16[24,208,256]{2,1,0:T(8,128)(2,1)S(1)}, bf16[24,208,256]{2,1,0:T(8,128)(2,1)S(1)}, f32[24,16,256]{2,1,0:T(8,128)S(1)}, f32[2,5,24,128]{3,2,1,0:T(8,128)S(1)}, s32[16,128]{1,0:T(8,128)S(4)}) custom-call(s32[1,48]{1,0:T(1,128)S(1)} %get-tuple-element.17.order_ref, f32[768,128]{1,0:T(8,128)S(1)} %get-tuple-element.18.vol_ref, ...), custom_call_target="tpu_custom_call" | custom-call | tf_op jit(solution)/shard_map/prepare/pallas_call | solution.py:605
  11.2 0.3 collective-permute-done.low_ref
  11.5 0.0 collective-permute-done.1.high_ref
  11.5 2.1 %first.1 = (f32[384,128]{1,0:T(8,128)S(1)}, f32[24,16,256]{2,1,0:T(8,128)S(1)}, f32[5,64,128]{2,1,0:T(8,128)S(1)}) custom-call(s32[16,128]{1,0:T(8,128)S(4)} %get-tuple-element.20.table_ref, bf16[24,208,256]{2,1,0:T(8,128)(2,1)S(1)} %get-tuple-element.21.w_ref.w0_ref, f32[24,16,256]{2,1,0:T(8,128)S(1)} %get-tuple-element.22.own_ref, ...), custom_call_target="tpu_custom_call" | custom-call | tf_op jit(solution)/shard_map/first/pallas_call | solution.py:557
  13.6 16.4 %all_to_all.20 = f32[32,3,4,128]{3,2,1,0:T(4,128)S(1)} all-to-all(f32[32,3,4,128]{3,2,1,0:T(4,128)S(1)} %bitcast.15), channel_id=1, replica_groups=mesh['gz'=8,'xy'=32] {'xy'}, dimensions={0} | all-to-all | bytes 393216 | tf_op jit(solution)/shard_map/all_to_all | solution.py:569
  30.0 0.8 %owner_a.1 = bf16[32,8,128]{2,1,0:T(8,128)(2,1)S(1)} custom-call(s32[16,128]{1,0:T(8,128)S(4)} %get-tuple-element.20.table_ref, f32[384,128]{1,0:T(8,128)S(1)} %bitcast.11), custom_call_target="tpu_custom_call" | custom-call | tf_op jit(solution)/shard_map/owner_a/pallas_call | solution.py:557
  30.8 10.9 %all_to_all.21.recv_ref = bf16[32,8,128]{2,1,0:T(8,128)(2,1)S(1)} all-to-all(bf16[32,8,128]{2,1,0:T(8,128)(2,1)S(1)} %owner_a.1), channel_id=1, replica_groups=mesh['gz'=8,'xy'=32] {'xy'}, dimensions={0} | all-to-all | bytes 131072 | tf_op jit(solution)/shard_map/all_to_all | solution.py:569
  41.7 2.3 %middle.1 = (f32[320,128]{1,0:T(8,128)S(1)}, f32[24,16,256]{2,1,0:T(8,128)S(1)}) custom-call(s32[16,128]{1,0:T(8,128)S(4)} %get-tuple-element.20.table_ref, bf16[32,8,128]{2,1,0:T(8,128)(2,1)S(1)} %all_to_all.21.recv_ref, f32[24,16,256]{2,1,0:T(8,128)S(1)} %get-tuple-element.22.own_ref, f32[24,16,256]{2,1,0:T(8,128)S(1)} %get-tuple-element.27.side_ref, ...), custom_call_target="tpu_custom_call" | custom-call | tf_op jit(solution)/shard_map/middle/pallas_call | solution.py:557
  44.1 11.5 %all_to_all.22 = f32[32,5,2,128]{3,2,1,0:T(2,128)S(1)} all-to-all(f32[32,5,2,128]{3,2,1,0:T(2,128)S(1)} %bitcast.16), channel_id=1, replica_groups=mesh['gz'=8,'xy'=32] {'xy'}, dimensions={0} | all-to-all | bytes 327680 | tf_op jit(solution)/shard_map/all_to_all | solution.py:569
  55.5 0.7 %owner_b.1 = f32[256,128]{1,0:T(8,128)S(1)} custom-call(s32[16,128]{1,0:T(8,128)S(4)} %get-tuple-element.20.table_ref, f32[320,128]{1,0:T(8,128)S(1)} %bitcast.12), custom_call_target="tpu_custom_call" | custom-call | tf_op jit(solution)/shard_map/owner_b/pallas_call | solution.py:557
  56.3 11.2 %all_to_all.23 = f32[32,8,128]{2,1,0:T(8,128)S(1)} all-to-all(f32[32,8,128]{2,1,0:T(8,128)S(1)} %bitcast.14), channel_id=1, replica_groups=mesh['gz'=8,'xy'=32] {'xy'}, dimensions={0} | all-to-all | bytes 262144 | tf_op jit(solution)/shard_map/all_to_all | solution.py:569
  67.5 2.4 %last.1 = (f32[16,48,128]{2,1,0:T(8,128)}, f32[5,20,48]{2,1,0:T(8,128)}) custom-call(s32[16,128]{1,0:T(8,128)S(4)} %get-tuple-element.20.table_ref, f32[256,128]{1,0:T(8,128)S(1)} %bitcast.13, f32[24,16,256]{2,1,0:T(8,128)S(1)} %get-tuple-element.31.old_ref, bf16[24,208,256]{2,1,0:T(8,128)(2,1)S(1)} %get-tuple-element.29.w1_ref.w_ref), custom_call_target="tpu_custom_call" | custom-call | tf_op jit(solution)/shard_map/last/pallas_call | solution.py:557
Async XLA Ops:
  1.8 9.7 %collective-permute-start = (bf16[512,128]{1,0:T(8,128)(2,1)S(1)}, bf16[512,128]{1,0:T(8,128)(2,1)S(1)}, u32[]{:S(2)}, u32[]{:S(2)}) collective-permute-start(bf16[512,128]{1,0:T(8,128)(2,1)S(1)} %get-tuple-element.24), channel_id=1, source_target_pairs={{0,32},{32,64},{64,96},{96,128},{128,160},{160,192},{192,224},{224... | collective-permute-start | bytes 393224 | tf_op jit(solution)/shard_map/ppermute | solution.py:603
  4.4 7.1 %collective-permute-start.1 = (bf16[512,128]{1,0:T(8,128)(2,1)S(1)}, bf16[512,128]{1,0:T(8,128)(2,1)S(1)}, u32[]{:S(2)}, u32[]{:S(2)}) collective-permute-start(bf16[512,128]{1,0:T(8,128)(2,1)S(1)} %get-tuple-element.25), channel_id=1, source_target_pairs={{32,0},{64,32},{96,64},{128,96},{160,128},{192,160},{224,192},{0,2... | collective-permute-start | bytes 393224 | tf_op jit(solution)/shard_map/ppermute | solution.py:604

commit v3 on v2

--- a/solution.py
+++ b/solution.py
@@ -31,6 +31,7 @@
 ONES = Z_ALL
 Z_PAD = 32
 GROUPS = 6
+GOT = GROUPS * 8
 ROWS_PER = (5, 4)
 ROWS_BELOW = (3, 0)
 M_HALO = 8
@@ -141,8 +142,9 @@
     return jnp.concatenate(pieces, axis=0).astype(jnp.bfloat16)
 
 
-def forward(w_ref, slices, acc_ref, m_ref, table_ref, out_ref, subset, gz):
-    acc_ref[...] = jnp.zeros_like(acc_ref)
+def forward(w_ref, slices, acc_refs, m_ref, table_ref, out_ref, subset, gz):
+    for acc_ref in acc_refs:
+        acc_ref[...] = jnp.zeros_like(acc_ref)
     for tile in range(TILES):
         offsets = tile_offsets(table_ref, subset, tile)
         part = lax.dot_general(
@@ -152,7 +154,7 @@
             preferred_element_type=jnp.float32,
         )
         for v in range(VIEWS):
-            acc_ref[v, pl.ds(offsets[v], COLS_TILE), :] += part[PLACE[v] : PLACE[v] + COLS_TILE]
+            acc_refs[v][pl.ds(offsets[v], COLS_TILE), :] += part[PLACE[v] : PLACE[v] + COLS_TILE]
     per = ROWS_PER[subset]
     half = per + 1
     size = GROUPS * 2 * half
@@ -171,7 +173,7 @@
     used = GROUPS * VIEWS * 2 * half
     out_ref[used:, :] = jnp.zeros((out_ref.shape[0] - used, 128), jnp.float32)
     for v in range(VIEWS):
-        sums = acc_ref[v]
+        sums = acc_refs[v][...]
         rounded = sums.astype(jnp.bfloat16).astype(jnp.float32)
         sums = jnp.where(left_over, sums - rounded, rounded).astype(jnp.bfloat16)
         sums = lax.dot_general(
@@ -184,20 +186,29 @@
         out_ref[v * size : (v + 1) * size, :] = part
 
 
+def three_parts(x, third):
+    first = x.astype(jnp.bfloat16).astype(jnp.float32)
+    second = (x - first).astype(jnp.bfloat16).astype(jnp.float32)
+    part = jnp.where(third == 0, first, jnp.where(third == 1, second, x - first - second))
+    return part.astype(jnp.bfloat16)
+
+
 def smear(recv_ref, sm_ref, gz):
-    i = iota((3 * Z_PAD, GROUPS * 8), 0)
-    k = iota((3 * Z_PAD, GROUPS * 8), 1)
+    i = iota((3 * Z_PAD, 3 * GOT), 0)
+    k = iota((3 * Z_PAD, 3 * GOT), 1)
+    third = (k >= GOT).astype(jnp.int32) + (k >= 2 * GOT).astype(jnp.int32)
+    k = k - GOT * third
     part = k & 7
-    third = i >> 5
-    slot = jnp.where(third == 0, part, 2 * (part - 5) + third - 1)
+    block = i >> 5
+    slot = jnp.where(block == 0, part, 2 * (part - 5) + block - 1)
     rows = slot_weights(k >> 3, slot, i & (Z_PAD - 1), gz, 0)
-    rows = jnp.where((third == 0) == (part < 5), rows, 0.0)
+    rows = three_parts(jnp.where((block == 0) == (part < 5), rows, 0.0), third)
     ones = iota((Z_PAD, LANES), 0) == ONES
     for v in range(VIEWS):
-        got = recv_ref[v * GROUPS : (v + 1) * GROUPS]
-        got = got.astype(jnp.float32).reshape(GROUPS * 8, 128)
+        got = recv_ref[v * GROUPS : (v + 1) * GROUPS].astype(jnp.float32)
+        got = got.reshape(GOT, 128).astype(jnp.bfloat16)
         sums = jnp.dot(
-            rows, got, precision=lax.Precision.HIGHEST, preferred_element_type=jnp.float32
+            rows, jnp.concatenate((got, got, got), axis=0), preferred_element_type=jnp.float32
         )
         high = sums[Z_PAD : 2 * Z_PAD] + pltpu.roll(sums[2 * Z_PAD :], 128 - COLS_DEV, 1)
         smeared = jnp.concatenate((sums[0:Z_PAD], high), axis=1)
@@ -206,22 +217,33 @@
 
 def smear_last(recv_ref, sm_ref, res_ref, gz):
     size = 2 * Z_PAD + 24
-    i = iota((size, GROUPS * 8), 0)
-    k = iota((size, GROUPS * 8), 1)
+    i = iota((size, 3 * GOT), 0)
+    k = iota((size, 3 * GOT), 1)
+    third = (k >= GOT).astype(jnp.int32) + (k >= 2 * GOT).astype(jnp.int32)
+    k = k - GOT * third
     part = k & 7
     rows = slot_weights(k >> 3, part & 3, i & (Z_PAD - 1), gz, 1)
-    rows = jnp.where((part >= 4) == (i >= Z_PAD), rows, 0.0)
+    rows = three_parts(jnp.where((part >= 4) == (i >= Z_PAD), rows, 0.0), third)
     j = i - 2 * Z_PAD + ((gz + 1) >> 1)
-    picked = (k == ((j >> 2) << 3) + 4 + (j & 3)).astype(jnp.float32)
-    rows = jnp.where(i >= 2 * Z_PAD, picked, rows)
+    picked = jnp.where(k == ((j >> 2) << 3) + 4 + (j & 3), 1.0, 0.0).astype(jnp.bfloat16)
+    rows = jnp.where(i >= 2 * Z_PAD, picked.astype(jnp.float32), rows.astype(jnp.float32))
+    rows = rows.astype(jnp.bfloat16)
     ones = iota((Z_PAD, LANES), 0) == ONES
-    part = iota((GROUPS * 8, 128), 0) & 7
-    exact = (part >= 4) & (iota((GROUPS * 8, 128), 1) >= MEAS_AT - 128)
+    part = iota((GOT, 128), 0) & 7
+    exact = (part >= 4) & (iota((GOT, 128), 1) >= MEAS_AT - 128)
     for v in range(VIEWS):
-        got = recv_ref[v * GROUPS * 8 : (v + 1) * GROUPS * 8, :]
-        got = jnp.where(exact, got, got.astype(jnp.bfloat16).astype(jnp.float32))
+        got = recv_ref[v * GOT : (v + 1) * GOT, :]
+        first = got.astype(jnp.bfloat16).astype(jnp.float32)
+        second = (got - first).astype(jnp.bfloat16).astype(jnp.float32)
+        parts = (
+            first,
+            jnp.where(exact, second, first),
+            jnp.where(exact, got - first - second, first),
+        )
         sums = jnp.dot(
-            rows, got, precision=lax.Precision.HIGHEST, preferred_element_type=jnp.float32
+            rows,
+            jnp.concatenate(parts, axis=0).astype(jnp.bfloat16),
+            preferred_element_type=jnp.float32,
         )
         smeared = jnp.concatenate((sums[0:Z_PAD], sums[Z_PAD : 2 * Z_PAD]), axis=1)
         sm_ref[v] = jnp.where(ones, 1.0, smeared).astype(jnp.bfloat16).astype(jnp.float32)
@@ -273,7 +295,7 @@
     return rows
 
 
-def relay(source_ref, out_ref, pitch):
+def relay(source_ref, out_ref, pitch, unrolled):
     def step(xb, nothing):
         for half in range(2):
             for b in range(2):
@@ -285,7 +307,11 @@
                     ] = block
         return nothing
 
-    lax.fori_loop(0, X_DEV // TILE, step, 0)
+    if unrolled:
+        for xb in range(X_DEV // TILE):
+            step(xb, 0)
+    else:
+        lax.fori_loop(0, X_DEV // TILE, step, 0)
 
 
 def pack_kernel(
@@ -336,7 +362,7 @@
     flat_ref[...], own = fill_table(cosine, sine, xy)
     copy = pltpu.make_async_copy(flat_ref, table_ref, sem)
     copy.start()
-    relay(vol_ref, own_ref, X_DEV)
+    relay(vol_ref, own_ref, X_DEV, False)
     mown_ref[...] = jnp.zeros_like(mown_ref)
     for s in range(SUBSETS):
         for v in range(VIEWS):
@@ -358,7 +384,7 @@
 
 def first_kernel(
     table_ref, w_ref, own_ref, mown_ref, low_ref, high_ref,
-    out_ref, side_ref, m1_ref, halo_ref, acc_ref, raw_ref, m0_ref, edge_ref,
+    out_ref, side_ref, m1_ref, halo_ref, raw_ref, m0_ref, edge_ref, *acc_refs,
 ):
     gz = lax.axis_index("gz")
     for side, (sent_ref, inner) in enumerate(((low_ref, Z_HALO // 2), (high_ref, 0))):
@@ -376,7 +402,7 @@
     for z in range(2 * Z_HALO, Z_DEV):
         value = 1.0 if z == ONES - Z_DEV else 0.0
         halo_ref[z * PITCH : z * PITCH + X_DEV, :] = jnp.full((X_DEV, NY), value, jnp.float32)
-    relay(halo_ref, side_ref, PITCH)
+    relay(halo_ref, side_ref, PITCH, True)
     for s, m_ref in ((0, m0_ref), (1, m1_ref)):
         per = ROWS_PER[s]
         m_ref[...] = jnp.zeros_like(m_ref)
@@ -402,12 +428,12 @@
     def slices(tile):
         return jnp.concatenate((own_ref[tile], side_ref[tile]), axis=0).astype(jnp.bfloat16)
 
-    forward(w_ref, slices, acc_ref, m0_ref, table_ref, out_ref, 0, gz)
+    forward(w_ref, slices, acc_refs, m0_ref, table_ref, out_ref, 0, gz)
 
 
 def middle_kernel(
     table_ref, recv_ref, own_ref, side_ref, m_ref, w0_ref, w1_ref,
-    out_ref, new_ref, sm_ref, vb_ref, acc_ref,
+    out_ref, new_ref, sm_ref, vb_ref, *acc_refs,
 ):
     gz = lax.axis_index("gz")
     smear(recv_ref, sm_ref, gz)
@@ -422,7 +448,7 @@
         vb_ref[tile] = new.astype(jnp.bfloat16)
 
     backward(w0_ref, sm_ref, table_ref, old, store, 0, gz)
-    forward(w1_ref, lambda tile: vb_ref[tile], acc_ref, m_ref, table_ref, out_ref, 1, gz)
+    forward(w1_ref, lambda tile: vb_ref[tile], acc_refs, m_ref, table_ref, out_ref, 1, gz)
 
 
 def last_kernel(
@@ -460,7 +486,7 @@
         copy.wait()
 
 
-def owner_kernel(table_ref, recv_ref, out_ref, acc_ref, sum_ref, mea_ref, *, subset):
+def owner_kernel(table_ref, recv_ref, out_ref, acc_ref, mea_ref, *sum_refs, subset):
     gz = lax.axis_index("gz")
     xy = lax.axis_index("xy")
     view = jnp.minimum(xy // GROUPS, VIEWS - 1)
@@ -469,7 +495,8 @@
     per = ROWS_PER[subset]
     half = per + 1
     lane = iota((8, 128), 1)
-    sum_ref[...] = jnp.zeros_like(sum_ref)
+    for sum_ref in sum_refs:
+        sum_ref[...] = jnp.zeros_like(sum_ref)
     mea_ref[...] = jnp.zeros_like(mea_ref)
     end = N_XY * 2 * half - 8
 
@@ -494,7 +521,7 @@
         low = pltpu.roll(recv_ref[row : row + 8, :], shift, 1)
         high = pltpu.roll(jnp.where(lane < WIN - 128, upper(s), 0.0), shift, 1)
         wrapped = lane < shift
-        part_ref = sum_ref.at[s % SUMS]
+        part_ref = sum_refs[s % SUMS]
         part_ref[:, pl.ds(base, 128)] += jnp.where(wrapped, 0.0, low)
         part_ref[:, pl.ds(base + 128, 128)] += jnp.where(wrapped, low, high)
         part_ref[:, pl.ds(base + 256, 128)] += jnp.where(wrapped, high, 0.0)
@@ -502,9 +529,9 @@
     row = first_row(gz, subset) + group * per + slot
     ray_rows = jnp.where(slot < per, hat(row, iota((8, NZ), 1)), 0.0)
     ray_rows = jnp.sum(ray_rows, axis=1, keepdims=True)
-    sums = sum_ref[0]
-    for part in range(1, SUMS):
-        sums = sums + sum_ref[part]
+    sums = sum_refs[0][...]
+    for part_ref in sum_refs[1:]:
+        sums = sums + part_ref[...]
     totals = sums[per : per + 1, :]
     acc_ref[...] = mea_ref[...] - sums / jnp.maximum(ray_rows * totals, 1.0)
     for t in range(N_XY):
@@ -582,9 +609,9 @@
     made = vmem((TILES, DEPTH, VOXELS), bf16)
     slices = vmem((TILES, Z_DEV, VOXELS), f32)
     sm_scratch = vmem((VIEWS, Z_PAD, LANES), f32)
-    acc_scratch = vmem((VIEWS, WIN, 128), f32)
+    acc_scratch = [vmem((WIN, 128), f32)] * VIEWS
     row_scratch = vmem((8, FULL), f32)
-    owner_scratch = [row_scratch, vmem((SUMS, 8, FULL), f32), row_scratch]
+    owner_scratch = [row_scratch] * (2 + SUMS)
 
     sent = vmem((SENT_ROWS, 128), bf16)
     hbm = pl.BlockSpec(memory_space=pltpu.HBM)
@@ -621,10 +648,10 @@
         [vmem((N_XY * 12, 128), f32), slices, vmem((VIEWS, 64, 128), f32)],
         [
             vmem((Z_DEV * PITCH, NY), f32),
-            acc_scratch,
             vmem((SUBSETS, VIEWS, M_ROWS, 128), f32),
             vmem((VIEWS, 72, 128), f32),
             vmem((2, EDGE_ROWS, 128), f32),
+            *acc_scratch,
         ],
         "first",
     )
@@ -639,7 +666,7 @@
         middle_kernel,
         (table, exchanged(rounded, rounded.shape), own, side, m1, w0, w1),
         [vmem((N_XY * 10, 128), f32), slices],
-        [sm_scratch, vmem((TILES, Z_PAD, VOXELS), bf16), acc_scratch],
+        [sm_scratch, vmem((TILES, Z_PAD, VOXELS), bf16), *acc_scratch],
         "middle",
     )
     (final,) = call(

time: 70.1 us -> 69.8 us (level)
  no operation moved by 1% of the time
where the time goes in v3:
time: 69.8 us; the launch traced here: 69.6 us
  blocking collectives  50 us (72%)
  Pallas kernels  12 us (17%)
  starting transfers between devices  6.56 us (9%)
    all_to_all x4, blocking collectives, exchanged(): lax.all_to_all(parts.reshape(shape), 'xy', split_axis=0, concat_axis=0, t...  50 us
    pallas_call x5, Pallas kernels, call(): pl.pallas_call(kernel, in_specs=[spec(x) for x in inputs], out_specs=[spe...  8.01 us
    ppermute x1, starting transfers between devices, local(): high = lax.ppermute(down, 'gz', [(j, i) for i, j in next_up])  4.03 us
    pallas_call x1, Pallas kernels, local(): pl.pallas_call(prepare_kernel, in_specs=[pl.BlockSpec(memory_space=vmem)]...  2.83 us
    ppermute x1, starting transfers between devices, local(): low = lax.ppermute(up, 'gz', next_up)  2.53 us
  transfers between devices with their start and end apart: 2, of which 1 were waited for; matrix products, arithmetic and copies ran while one was open for 0% of the time, Pallas kernels for 4%

profile of v3, /device:TPU:1, one launch (start us, length us, event | category | flops | bytes accessed | tf_op | source)
XLA Modules:
  0.0 69.6 jit_solution(15803792854646247479)
XLA Ops:
  0.6 1.2 %pack.1 = (bf16[512,128]{1,0:T(8,128)(2,1)S(1)}, bf16[512,128]{1,0:T(8,128)(2,1)S(1)}, f32[768,128]{1,0:T(8,128)S(1)}, f32[200,48]{1,0:T(8,128)S(1)}, s32[1,48]{1,0:T(1,128)S(1)}) custom-call(f32[768,128]{1,0:T(8,128)} %bitcast.17, f32[200,48]{1,0:T(8,128)} %bitcast.18, s32[1,48]{1,0:T(1,128)} %bitcast.19), custom_call_target="tpu_custom_call" | custom-call | tf_op jit(solution)/shard_map/pack/pallas_call | solution.py:618
  1.8 2.5 %collective-permute-start = (bf16[512,128]{1,0:T(8,128)(2,1)S(1)}, bf16[512,128]{1,0:T(8,128)(2,1)S(1)}, u32[]{:S(2)}, u32[]{:S(2)}) collective-permute-start(bf16[512,128]{1,0:T(8,128)(2,1)S(1)} %get-tuple-element.24), channel_id=1, source_target_pairs={{0,32},{32,64},{64,96},{96,128},{128,160},{160,192},{192,224},{224... | collective-permute-start | bytes 393224 | tf_op jit(solution)/shard_map/ppermute | solution.py:630
  4.4 4.0 %collective-permute-start.1 = (bf16[512,128]{1,0:T(8,128)(2,1)S(1)}, bf16[512,128]{1,0:T(8,128)(2,1)S(1)}, u32[]{:S(2)}, u32[]{:S(2)}) collective-permute-start(bf16[512,128]{1,0:T(8,128)(2,1)S(1)} %get-tuple-element.25), channel_id=1, source_target_pairs={{32,0},{64,32},{96,64},{128,96},{160,128},{192,160},{224,192},{0,2... | collective-permute-start | bytes 393224 | tf_op jit(solution)/shard_map/ppermute | solution.py:631
  8.4 2.8 %prepare.1 = (bf16[24,208,256]{2,1,0:T(8,128)(2,1)S(1)}, bf16[24,208,256]{2,1,0:T(8,128)(2,1)S(1)}, f32[24,16,256]{2,1,0:T(8,128)S(1)}, f32[2,5,24,128]{3,2,1,0:T(8,128)S(1)}, s32[16,128]{1,0:T(8,128)S(4)}) custom-call(s32[1,48]{1,0:T(1,128)S(1)} %get-tuple-element.17.order_ref, f32[768,128]{1,0:T(8,128)S(1)} %get-tuple-element.18.vol_ref, ...), custom_call_target="tpu_custom_call" | custom-call | tf_op jit(solution)/shard_map/prepare/pallas_call | solution.py:632
  11.2 0.3 collective-permute-done.low_ref
  11.5 0.0 collective-permute-done.1.high_ref
  11.5 1.8 %first.1 = (f32[384,128]{1,0:T(8,128)S(1)}, f32[24,16,256]{2,1,0:T(8,128)S(1)}, f32[5,64,128]{2,1,0:T(8,128)S(1)}) custom-call(s32[16,128]{1,0:T(8,128)S(4)} %get-tuple-element.20.table_ref, bf16[24,208,256]{2,1,0:T(8,128)(2,1)S(1)} %get-tuple-element.21.w_ref.w0_ref, f32[24,16,256]{2,1,0:T(8,128)S(1)} %get-tuple-element.22.own_ref, ...), custom_call_target="tpu_custom_call" | custom-call | tf_op jit(solution)/shard_map/first/pallas_call | solution.py:584
  13.4 16.4 %all_to_all.20 = f32[32,3,4,128]{3,2,1,0:T(4,128)S(1)} all-to-all(f32[32,3,4,128]{3,2,1,0:T(4,128)S(1)} %bitcast.15), channel_id=1, replica_groups=mesh['gz'=8,'xy'=32] {'xy'}, dimensions={0} | all-to-all | bytes 393216 | tf_op jit(solution)/shard_map/all_to_all | solution.py:596
  29.8 0.6 owner_a.1
  30.3 10.9 %all_to_all.21.recv_ref = bf16[32,8,128]{2,1,0:T(8,128)(2,1)S(1)} all-to-all(bf16[32,8,128]{2,1,0:T(8,128)(2,1)S(1)} %owner_a.1), channel_id=1, replica_groups=mesh['gz'=8,'xy'=32] {'xy'}, dimensions={0} | all-to-all | bytes 131072 | tf_op jit(solution)/shard_map/all_to_all | solution.py:596
  41.2 2.2 %middle.1 = (f32[320,128]{1,0:T(8,128)S(1)}, f32[24,16,256]{2,1,0:T(8,128)S(1)}) custom-call(s32[16,128]{1,0:T(8,128)S(4)} %get-tuple-element.20.table_ref, bf16[32,8,128]{2,1,0:T(8,128)(2,1)S(1)} %all_to_all.21.recv_ref, f32[24,16,256]{2,1,0:T(8,128)S(1)} %get-tuple-element.22.own_ref, f32[24,16,256]{2,1,0:T(8,128)S(1)} %get-tuple-element.27.side_ref, ...), custom_call_target="tpu_custom_call" | custom-call | tf_op jit(solution)/shard_map/middle/pallas_call | solution.py:584
  43.4 11.5 %all_to_all.22 = f32[32,5,2,128]{3,2,1,0:T(2,128)S(1)} all-to-all(f32[32,5,2,128]{3,2,1,0:T(2,128)S(1)} %bitcast.16), channel_id=1, replica_groups=mesh['gz'=8,'xy'=32] {'xy'}, dimensions={0} | all-to-all | bytes 327680 | tf_op jit(solution)/shard_map/all_to_all | solution.py:596
  54.9 0.5 owner_b.1
  55.4 11.2 %all_to_all.23 = f32[32,8,128]{2,1,0:T(8,128)S(1)} all-to-all(f32[32,8,128]{2,1,0:T(8,128)S(1)} %bitcast.14), channel_id=1, replica_groups=mesh['gz'=8,'xy'=32] {'xy'}, dimensions={0} | all-to-all | bytes 262144 | tf_op jit(solution)/shard_map/all_to_all | solution.py:596
  66.7 2.9 %last.1 = (f32[16,48,128]{2,1,0:T(8,128)}, f32[5,20,48]{2,1,0:T(8,128)}) custom-call(s32[16,128]{1,0:T(8,128)S(4)} %get-tuple-element.20.table_ref, f32[256,128]{1,0:T(8,128)S(1)} %bitcast.13, f32[24,16,256]{2,1,0:T(8,128)S(1)} %get-tuple-element.31.old_ref, bf16[24,208,256]{2,1,0:T(8,128)(2,1)S(1)} %get-tuple-element.29.w1_ref.w_ref), custom_call_target="tpu_custom_call" | custom-call | tf_op jit(solution)/shard_map/last/pallas_call | solution.py:584
Async XLA Ops:
  1.8 9.7 %collective-permute-start = (bf16[512,128]{1,0:T(8,128)(2,1)S(1)}, bf16[512,128]{1,0:T(8,128)(2,1)S(1)}, u32[]{:S(2)}, u32[]{:S(2)}) collective-permute-start(bf16[512,128]{1,0:T(8,128)(2,1)S(1)} %get-tuple-element.24), channel_id=1, source_target_pairs={{0,32},{32,64},{64,96},{96,128},{128,160},{160,192},{192,224},{224... | collective-permute-start | bytes 393224 | tf_op jit(solution)/shard_map/ppermute | solution.py:630
  4.4 7.1 %collective-permute-start.1 = (bf16[512,128]{1,0:T(8,128)(2,1)S(1)}, bf16[512,128]{1,0:T(8,128)(2,1)S(1)}, u32[]{:S(2)}, u32[]{:S(2)}) collective-permute-start(bf16[512,128]{1,0:T(8,128)(2,1)S(1)} %get-tuple-element.25), channel_id=1, source_target_pairs={{32,0},{64,32},{96,64},{128,96},{160,128},{192,160},{224,192},{0,2... | collective-permute-start | bytes 393224 | tf_op jit(solution)/shard_map/ppermute | solution.py:631

commit v4 on v3

--- a/solution.py
+++ b/solution.py
@@ -51,8 +51,6 @@
 EDGE_AT = HALO_ROWS + INNER_ROWS
 EDGE_ROWS = SUBSETS * VIEWS * M_HALO
 SENT_ROWS = EDGE_AT + EDGE_ROWS
-PITCH = 56
-OUT_PITCH = 24
 TABLE = (16, 128)
 SHIFT_AT = 32
 TILE_AT = 64
@@ -281,26 +279,33 @@
         store(tile, old(tile), back / jnp.maximum(norm, 1.0))
 
 
-def swap_blocks(rows):
-    block = iota((8, 128), 1) >> 4
+def swapped(rows, index, turn, axis):
     for d in (4, 2, 1):
-        high = (block & d) != 0
+        high = (index & d) != 0
         new = list(rows)
         for i in range(8):
             if i & d == 0:
                 a, b = (rows[i], rows[i + d])
-                new[i] = jnp.where(high, pltpu.roll(b, 16 * d, 1), a)
-                new[i + d] = jnp.where(high, b, pltpu.roll(a, 128 - 16 * d, 1))
+                new[i] = jnp.where(high, pltpu.roll(b, turn * d, axis), a)
+                new[i + d] = jnp.where(high, b, pltpu.roll(a, turn * (8 - d), axis))
         rows = new
     return rows
 
 
-def relay(source_ref, out_ref, pitch, unrolled):
+def swap_blocks(rows):
+    return swapped(rows, iota((8, 128), 1) >> 4, 16, 1)
+
+
+def swap_sublanes(rows):
+    return swapped(rows, iota((8, 128), 0), 1, 0)
+
+
+def relay(read, out_ref, unrolled):
     def step(xb, nothing):
         for half in range(2):
             for b in range(2):
-                at = xb * TILE + half * 8 + b * 8 * pitch
-                rows = [source_ref[pl.ds(at + i, 8, stride=pitch), :] for i in range(8)]
+                x = xb * TILE + half * 8
+                rows = swap_sublanes([read(b * 8 + z, x) for z in range(8)])
                 for q, block in enumerate(swap_blocks(rows)):
                     out_ref[
                         xb * TILES_Y + q, b * 8 : b * 8 + 8, half * 128 : half * 128 + 128
@@ -362,7 +367,9 @@
     flat_ref[...], own = fill_table(cosine, sine, xy)
     copy = pltpu.make_async_copy(flat_ref, table_ref, sem)
     copy.start()
-    relay(vol_ref, own_ref, X_DEV, False)
+    relay(
+        lambda z, x: vol_ref[pl.ds(pl.multiple_of(z * X_DEV + x, 8), 8), :], own_ref, False
+    )
     mown_ref[...] = jnp.zeros_like(mown_ref)
     for s in range(SUBSETS):
         for v in range(VIEWS):
@@ -384,25 +391,27 @@
 
 def first_kernel(
     table_ref, w_ref, own_ref, mown_ref, low_ref, high_ref,
-    out_ref, side_ref, m1_ref, halo_ref, raw_ref, m0_ref, edge_ref, *acc_refs,
+    out_ref, side_ref, m1_ref, raw_ref, m0_ref, edge_ref, *acc_refs,
 ):
     gz = lax.axis_index("gz")
-    for side, (sent_ref, inner) in enumerate(((low_ref, Z_HALO // 2), (high_ref, 0))):
-        left_at = HALO_ROWS - inner * X_DEV
-        for z in range(Z_HALO):
-            at = z * X_DEV
-            rows = sent_ref[at : at + X_DEV, :].astype(jnp.float32)
-            if inner <= z < inner + Z_HALO // 2:
-                rows = rows + sent_ref[left_at + at : left_at + at + X_DEV, :].astype(jnp.float32)
-            at = (side * Z_HALO + z) * PITCH
-            halo_ref[at : at + X_DEV, :] = rows
+    for side, sent_ref in enumerate((low_ref, high_ref)):
         edge = sent_ref[EDGE_AT:SENT_ROWS, :].astype(jnp.float32)
         edge = edge + pltpu.roll(edge, COLS_DEV, 1)
         edge_ref[side] = jnp.where(iota(edge.shape, 1) >= MEAS_AT - 128, edge, 0.0)
-    for z in range(2 * Z_HALO, Z_DEV):
-        value = 1.0 if z == ONES - Z_DEV else 0.0
-        halo_ref[z * PITCH : z * PITCH + X_DEV, :] = jnp.full((X_DEV, NY), value, jnp.float32)
-    relay(halo_ref, side_ref, PITCH, True)
+
+    def read(z, x):
+        if z >= 2 * Z_HALO:
+            return jnp.full((8, NY), 1.0 if z == ONES - Z_DEV else 0.0, jnp.float32)
+        sent_ref, inner = (low_ref, Z_HALO // 2) if z < Z_HALO else (high_ref, 0)
+        z = z % Z_HALO
+        at = z * X_DEV + x
+        rows = sent_ref[at : at + 8, :].astype(jnp.float32)
+        if inner <= z < inner + Z_HALO // 2:
+            at = at + HALO_ROWS - inner * X_DEV
+            rows = rows + sent_ref[at : at + 8, :].astype(jnp.float32)
+        return rows
+
+    relay(read, side_ref, True)
     for s, m_ref in ((0, m0_ref), (1, m1_ref)):
         per = ROWS_PER[s]
         m_ref[...] = jnp.zeros_like(m_ref)
@@ -471,14 +480,13 @@
                     new_ref[xb * TILES_Y + q, b * 8 : b * 8 + 8, half * 128 : half * 128 + 128]
                     for q in range(TILES_Y)
                 ]
-                at = half * 8 + b * 8 * OUT_PITCH
-                for i, row in enumerate(swap_blocks(blocks)):
-                    block_ref[xb, pl.ds(at + i, 8, stride=OUT_PITCH), :] = row
+                x = xb * TILE + half * 8
+                for z, row in enumerate(swap_sublanes(swap_blocks(blocks))):
+                    block_ref[b * 8 + z, x : x + 8, :] = row
+        columns = pl.ds(xb * TILE, TILE)
         copies.append(
             pltpu.make_async_copy(
-                block_ref.at[xb].reshape(Z_DEV, OUT_PITCH, NY).at[:, 0:TILE, :],
-                out_ref.at[:, pl.ds(xb * TILE, TILE), :],
-                sems.at[xb],
+                block_ref.at[:, columns, :], out_ref.at[:, columns, :], sems.at[xb]
             )
         )
         copies[-1].start()
@@ -647,7 +655,6 @@
         (table, w0, own, mown, low, high),
         [vmem((N_XY * 12, 128), f32), slices, vmem((VIEWS, 64, 128), f32)],
         [
-            vmem((Z_DEV * PITCH, NY), f32),
             vmem((SUBSETS, VIEWS, M_ROWS, 128), f32),
             vmem((VIEWS, 72, 128), f32),
             vmem((2, EDGE_ROWS, 128), f32),
@@ -686,7 +693,7 @@
         [
             sm_scratch,
             slices,
-            vmem((X_DEV // TILE, Z_DEV * OUT_PITCH, NY), f32),
+            vmem(VOLUME, f32),
             vmem((VIEWS, ROWS_DEV, COLS_DEV), f32),
             pltpu.SemaphoreType.DMA((X_DEV // TILE + 1,)),
         ],

time: 69.8 us -> 69.7 us (level)
  no operation moved by 1% of the time
where the time goes in v4:
time: 69.7 us; the launch traced here: 69.5 us
  blocking collectives  50.1 us (72%)
  Pallas kernels  11.9 us (17%)
  starting transfers between devices  6.56 us (9%)
    all_to_all x4, blocking collectives, exchanged(): lax.all_to_all(parts.reshape(shape), 'xy', split_axis=0, concat_axis=0, t...  50.1 us
    pallas_call x5, Pallas kernels, call(): pl.pallas_call(kernel, in_specs=[spec(x) for x in inputs], out_specs=[spe...  7.86 us
    ppermute x1, starting transfers between devices, local(): high = lax.ppermute(down, 'gz', [(j, i) for i, j in next_up])  4.03 us
    pallas_call x1, Pallas kernels, local(): pl.pallas_call(prepare_kernel, in_specs=[pl.BlockSpec(memory_space=vmem)]...  2.84 us
    ppermute x1, starting transfers between devices, local(): low = lax.ppermute(up, 'gz', next_up)  2.53 us
  transfers between devices with their start and end apart: 2, of which 1 were waited for; matrix products, arithmetic and copies ran while one was open for 0% of the time, Pallas kernels for 4%

profile of v4, /device:TPU:1, one launch (start us, length us, event | category | flops | bytes accessed | tf_op | source)
XLA Modules:
  0.0 69.5 jit_solution(8257165966455730608)
XLA Ops:
  0.6 1.2 %pack.1 = (bf16[512,128]{1,0:T(8,128)(2,1)S(1)}, bf16[512,128]{1,0:T(8,128)(2,1)S(1)}, f32[768,128]{1,0:T(8,128)S(1)}, f32[200,48]{1,0:T(8,128)S(1)}, s32[1,48]{1,0:T(1,128)S(1)}) custom-call(f32[768,128]{1,0:T(8,128)} %bitcast.17, f32[200,48]{1,0:T(8,128)} %bitcast.18, s32[1,48]{1,0:T(1,128)} %bitcast.19), custom_call_target="tpu_custom_call" | custom-call | tf_op jit(solution)/shard_map/pack/pallas_call | solution.py:626
  1.8 2.5 %collective-permute-start = (bf16[512,128]{1,0:T(8,128)(2,1)S(1)}, bf16[512,128]{1,0:T(8,128)(2,1)S(1)}, u32[]{:S(2)}, u32[]{:S(2)}) collective-permute-start(bf16[512,128]{1,0:T(8,128)(2,1)S(1)} %get-tuple-element.24), channel_id=1, source_target_pairs={{0,32},{32,64},{64,96},{96,128},{128,160},{160,192},{192,224},{224... | collective-permute-start | bytes 393224 | tf_op jit(solution)/shard_map/ppermute | solution.py:638
  4.4 4.0 %collective-permute-start.1 = (bf16[512,128]{1,0:T(8,128)(2,1)S(1)}, bf16[512,128]{1,0:T(8,128)(2,1)S(1)}, u32[]{:S(2)}, u32[]{:S(2)}) collective-permute-start(bf16[512,128]{1,0:T(8,128)(2,1)S(1)} %get-tuple-element.25), channel_id=1, source_target_pairs={{32,0},{64,32},{96,64},{128,96},{160,128},{192,160},{224,192},{0,2... | collective-permute-start | bytes 393224 | tf_op jit(solution)/shard_map/ppermute | solution.py:639
  8.4 2.8 %prepare.1 = (bf16[24,208,256]{2,1,0:T(8,128)(2,1)S(1)}, bf16[24,208,256]{2,1,0:T(8,128)(2,1)S(1)}, f32[24,16,256]{2,1,0:T(8,128)S(1)}, f32[2,5,24,128]{3,2,1,0:T(8,128)S(1)}, s32[16,128]{1,0:T(8,128)S(4)}) custom-call(s32[1,48]{1,0:T(1,128)S(1)} %get-tuple-element.17.order_ref, f32[768,128]{1,0:T(8,128)S(1)} %get-tuple-element.18.vol_ref, ...), custom_call_target="tpu_custom_call" | custom-call | tf_op jit(solution)/shard_map/prepare/pallas_call | solution.py:640
  11.2 0.3 collective-permute-done.low_ref
  11.5 0.0 collective-permute-done.1.high_ref
  11.5 1.8 %first.1 = (f32[384,128]{1,0:T(8,128)S(1)}, f32[24,16,256]{2,1,0:T(8,128)S(1)}, f32[5,64,128]{2,1,0:T(8,128)S(1)}) custom-call(s32[16,128]{1,0:T(8,128)S(4)} %get-tuple-element.20.table_ref, bf16[24,208,256]{2,1,0:T(8,128)(2,1)S(1)} %get-tuple-element.21.w_ref.w0_ref, f32[24,16,256]{2,1,0:T(8,128)S(1)} %get-tuple-element.22.own_ref, ...), custom_call_target="tpu_custom_call" | custom-call | tf_op jit(solution)/shard_map/first/pallas_call | solution.py:592
  13.3 16.4 %all_to_all.20 = f32[32,3,4,128]{3,2,1,0:T(4,128)S(1)} all-to-all(f32[32,3,4,128]{3,2,1,0:T(4,128)S(1)} %bitcast.15), channel_id=1, replica_groups=mesh['gz'=8,'xy'=32] {'xy'}, dimensions={0} | all-to-all | bytes 393216 | tf_op jit(solution)/shard_map/all_to_all | solution.py:604
  29.7 0.6 owner_a.1
  30.3 10.9 %all_to_all.21.recv_ref = bf16[32,8,128]{2,1,0:T(8,128)(2,1)S(1)} all-to-all(bf16[32,8,128]{2,1,0:T(8,128)(2,1)S(1)} %owner_a.1), channel_id=1, replica_groups=mesh['gz'=8,'xy'=32] {'xy'}, dimensions={0} | all-to-all | bytes 131072 | tf_op jit(solution)/shard_map/all_to_all | solution.py:604
  41.2 2.2 %middle.1 = (f32[320,128]{1,0:T(8,128)S(1)}, f32[24,16,256]{2,1,0:T(8,128)S(1)}) custom-call(s32[16,128]{1,0:T(8,128)S(4)} %get-tuple-element.20.table_ref, bf16[32,8,128]{2,1,0:T(8,128)(2,1)S(1)} %all_to_all.21.recv_ref, f32[24,16,256]{2,1,0:T(8,128)S(1)} %get-tuple-element.22.own_ref, f32[24,16,256]{2,1,0:T(8,128)S(1)} %get-tuple-element.27.side_ref, ...), custom_call_target="tpu_custom_call" | custom-call | tf_op jit(solution)/shard_map/middle/pallas_call | solution.py:592
  43.4 11.5 %all_to_all.22 = f32[32,5,2,128]{3,2,1,0:T(2,128)S(1)} all-to-all(f32[32,5,2,128]{3,2,1,0:T(2,128)S(1)} %bitcast.16), channel_id=1, replica_groups=mesh['gz'=8,'xy'=32] {'xy'}, dimensions={0} | all-to-all | bytes 327680 | tf_op jit(solution)/shard_map/all_to_all | solution.py:604
  54.8 0.5 owner_b.1
  55.3 11.2 %all_to_all.23 = f32[32,8,128]{2,1,0:T(8,128)S(1)} all-to-all(f32[32,8,128]{2,1,0:T(8,128)S(1)} %bitcast.14), channel_id=1, replica_groups=mesh['gz'=8,'xy'=32] {'xy'}, dimensions={0} | all-to-all | bytes 262144 | tf_op jit(solution)/shard_map/all_to_all | solution.py:604
  66.6 2.9 %last.1 = (f32[16,48,128]{2,1,0:T(8,128)}, f32[5,20,48]{2,1,0:T(8,128)}) custom-call(s32[16,128]{1,0:T(8,128)S(4)} %get-tuple-element.20.table_ref, f32[256,128]{1,0:T(8,128)S(1)} %bitcast.13, f32[24,16,256]{2,1,0:T(8,128)S(1)} %get-tuple-element.31.old_ref, bf16[24,208,256]{2,1,0:T(8,128)(2,1)S(1)} %get-tuple-element.29.w1_ref.w_ref), custom_call_target="tpu_custom_call" | custom-call | tf_op jit(solution)/shard_map/last/pallas_call | solution.py:592
Async XLA Ops:
  1.8 9.7 %collective-permute-start = (bf16[512,128]{1,0:T(8,128)(2,1)S(1)}, bf16[512,128]{1,0:T(8,128)(2,1)S(1)}, u32[]{:S(2)}, u32[]{:S(2)}) collective-permute-start(bf16[512,128]{1,0:T(8,128)(2,1)S(1)} %get-tuple-element.24), channel_id=1, source_target_pairs={{0,32},{32,64},{64,96},{96,128},{128,160},{160,192},{192,224},{224... | collective-permute-start | bytes 393224 | tf_op jit(solution)/shard_map/ppermute | solution.py:638
  4.4 7.1 %collective-permute-start.1 = (bf16[512,128]{1,0:T(8,128)(2,1)S(1)}, bf16[512,128]{1,0:T(8,128)(2,1)S(1)}, u32[]{:S(2)}, u32[]{:S(2)}) collective-permute-start(bf16[512,128]{1,0:T(8,128)(2,1)S(1)} %get-tuple-element.25), channel_id=1, source_target_pairs={{32,0},{64,32},{96,64},{128,96},{160,128},{192,160},{224,192},{0,2... | collective-permute-start | bytes 393224 | tf_op jit(solution)/shard_map/ppermute | solution.py:639

commit v5 on v4

--- a/solution.py
+++ b/solution.py
@@ -471,9 +471,9 @@
 
     def store(tile, old, change):
         new_ref[tile] = old + change[0:Z_DEV]
-
-    backward(w_ref, sm_ref, table_ref, lambda tile: old_ref[tile], store, 1, gz)
-    for xb in range(X_DEV // TILE):
+        xb = tile // TILES_Y
+        if tile % TILES_Y < TILES_Y - 1:
+            return
         for half in range(2):
             for b in range(Z_DEV // 8):
                 blocks = [
@@ -490,6 +490,8 @@
             )
         )
         copies[-1].start()
+
+    backward(w_ref, sm_ref, table_ref, lambda tile: old_ref[tile], store, 1, gz)
     for copy in copies:
         copy.wait()
 

time: 69.7 us -> 69 us (0.990)
  Pallas kernels: 11.9 us -> 11.2 us
where the time goes in v5:
time: 69 us; the launch traced here: 68.8 us
  blocking collectives  50.1 us (73%)
  Pallas kernels  11.2 us (16%)
  starting transfers between devices  6.56 us (10%)
    all_to_all x4, blocking collectives, exchanged(): lax.all_to_all(parts.reshape(shape), 'xy', split_axis=0, concat_axis=0, t...  50.1 us
    pallas_call x5, Pallas kernels, call(): pl.pallas_call(kernel, in_specs=[spec(x) for x in inputs], out_specs=[spe...  7.18 us
    ppermute x1, starting transfers between devices, local(): high = lax.ppermute(down, 'gz', [(j, i) for i, j in next_up])  4.03 us
    pallas_call x1, Pallas kernels, local(): pl.pallas_call(prepare_kernel, in_specs=[pl.BlockSpec(memory_space=vmem)]...  2.84 us
    ppermute x1, starting transfers between devices, local(): low = lax.ppermute(up, 'gz', next_up)  2.53 us
  transfers between devices with their start and end apart: 2, of which 1 were waited for; matrix products, arithmetic and copies ran while one was open for 0% of the time, Pallas kernels for 4%

profile of v5, /device:TPU:1, one launch (start us, length us, event | category | flops | bytes accessed | tf_op | source)
XLA Modules:
  0.0 68.8 jit_solution(1861928967361271782)
XLA Ops:
  0.6 1.2 %pack.1 = (bf16[512,128]{1,0:T(8,128)(2,1)S(1)}, bf16[512,128]{1,0:T(8,128)(2,1)S(1)}, f32[768,128]{1,0:T(8,128)S(1)}, f32[200,48]{1,0:T(8,128)S(1)}, s32[1,48]{1,0:T(1,128)S(1)}) custom-call(f32[768,128]{1,0:T(8,128)} %bitcast.17, f32[200,48]{1,0:T(8,128)} %bitcast.18, s32[1,48]{1,0:T(1,128)} %bitcast.19), custom_call_target="tpu_custom_call" | custom-call | tf_op jit(solution)/shard_map/pack/pallas_call | solution.py:628
  1.8 2.5 %collective-permute-start = (bf16[512,128]{1,0:T(8,128)(2,1)S(1)}, bf16[512,128]{1,0:T(8,128)(2,1)S(1)}, u32[]{:S(2)}, u32[]{:S(2)}) collective-permute-start(bf16[512,128]{1,0:T(8,128)(2,1)S(1)} %get-tuple-element.24), channel_id=1, source_target_pairs={{0,32},{32,64},{64,96},{96,128},{128,160},{160,192},{192,224},{224... | collective-permute-start | bytes 393224 | tf_op jit(solution)/shard_map/ppermute | solution.py:640
  4.4 4.0 %collective-permute-start.1 = (bf16[512,128]{1,0:T(8,128)(2,1)S(1)}, bf16[512,128]{1,0:T(8,128)(2,1)S(1)}, u32[]{:S(2)}, u32[]{:S(2)}) collective-permute-start(bf16[512,128]{1,0:T(8,128)(2,1)S(1)} %get-tuple-element.25), channel_id=1, source_target_pairs={{32,0},{64,32},{96,64},{128,96},{160,128},{192,160},{224,192},{0,2... | collective-permute-start | bytes 393224 | tf_op jit(solution)/shard_map/ppermute | solution.py:641
  8.4 2.8 %prepare.1 = (bf16[24,208,256]{2,1,0:T(8,128)(2,1)S(1)}, bf16[24,208,256]{2,1,0:T(8,128)(2,1)S(1)}, f32[24,16,256]{2,1,0:T(8,128)S(1)}, f32[2,5,24,128]{3,2,1,0:T(8,128)S(1)}, s32[16,128]{1,0:T(8,128)S(4)}) custom-call(s32[1,48]{1,0:T(1,128)S(1)} %get-tuple-element.17.order_ref, f32[768,128]{1,0:T(8,128)S(1)} %get-tuple-element.18.vol_ref, ...), custom_call_target="tpu_custom_call" | custom-call | tf_op jit(solution)/shard_map/prepare/pallas_call | solution.py:642
  11.2 0.3 collective-permute-done.low_ref
  11.5 0.0 collective-permute-done.1.high_ref
  11.5 1.8 %first.1 = (f32[384,128]{1,0:T(8,128)S(1)}, f32[24,16,256]{2,1,0:T(8,128)S(1)}, f32[5,64,128]{2,1,0:T(8,128)S(1)}) custom-call(s32[16,128]{1,0:T(8,128)S(4)} %get-tuple-element.20.table_ref, bf16[24,208,256]{2,1,0:T(8,128)(2,1)S(1)} %get-tuple-element.21.w_ref.w0_ref, f32[24,16,256]{2,1,0:T(8,128)S(1)} %get-tuple-element.22.own_ref, ...), custom_call_target="tpu_custom_call" | custom-call | tf_op jit(solution)/shard_map/first/pallas_call | solution.py:594
  13.3 16.4 %all_to_all.20 = f32[32,3,4,128]{3,2,1,0:T(4,128)S(1)} all-to-all(f32[32,3,4,128]{3,2,1,0:T(4,128)S(1)} %bitcast.15), channel_id=1, replica_groups=mesh['gz'=8,'xy'=32] {'xy'}, dimensions={0} | all-to-all | bytes 393216 | tf_op jit(solution)/shard_map/all_to_all | solution.py:606
  29.7 0.6 owner_a.1
  30.3 10.9 %all_to_all.21.recv_ref = bf16[32,8,128]{2,1,0:T(8,128)(2,1)S(1)} all-to-all(bf16[32,8,128]{2,1,0:T(8,128)(2,1)S(1)} %owner_a.1), channel_id=1, replica_groups=mesh['gz'=8,'xy'=32] {'xy'}, dimensions={0} | all-to-all | bytes 131072 | tf_op jit(solution)/shard_map/all_to_all | solution.py:606
  41.2 2.2 %middle.1 = (f32[320,128]{1,0:T(8,128)S(1)}, f32[24,16,256]{2,1,0:T(8,128)S(1)}) custom-call(s32[16,128]{1,0:T(8,128)S(4)} %get-tuple-element.20.table_ref, bf16[32,8,128]{2,1,0:T(8,128)(2,1)S(1)} %all_to_all.21.recv_ref, f32[24,16,256]{2,1,0:T(8,128)S(1)} %get-tuple-element.22.own_ref, f32[24,16,256]{2,1,0:T(8,128)S(1)} %get-tuple-element.27.side_ref, ...), custom_call_target="tpu_custom_call" | custom-call | tf_op jit(solution)/shard_map/middle/pallas_call | solution.py:594
  43.4 11.5 %all_to_all.22 = f32[32,5,2,128]{3,2,1,0:T(2,128)S(1)} all-to-all(f32[32,5,2,128]{3,2,1,0:T(2,128)S(1)} %bitcast.16), channel_id=1, replica_groups=mesh['gz'=8,'xy'=32] {'xy'}, dimensions={0} | all-to-all | bytes 327680 | tf_op jit(solution)/shard_map/all_to_all | solution.py:606
  54.8 0.5 owner_b.1
  55.4 11.2 %all_to_all.23 = f32[32,8,128]{2,1,0:T(8,128)S(1)} all-to-all(f32[32,8,128]{2,1,0:T(8,128)S(1)} %bitcast.14), channel_id=1, replica_groups=mesh['gz'=8,'xy'=32] {'xy'}, dimensions={0} | all-to-all | bytes 262144 | tf_op jit(solution)/shard_map/all_to_all | solution.py:606
  66.6 2.2 %last.1 = (f32[16,48,128]{2,1,0:T(8,128)}, f32[5,20,48]{2,1,0:T(8,128)}) custom-call(s32[16,128]{1,0:T(8,128)S(4)} %get-tuple-element.20.table_ref, f32[256,128]{1,0:T(8,128)S(1)} %bitcast.13, f32[24,16,256]{2,1,0:T(8,128)S(1)} %get-tuple-element.31.old_ref, bf16[24,208,256]{2,1,0:T(8,128)(2,1)S(1)} %get-tuple-element.29.w1_ref.w_ref), custom_call_target="tpu_custom_call" | custom-call | tf_op jit(solution)/shard_map/last/pallas_call | solution.py:594
Async XLA Ops:
  1.8 9.7 %collective-permute-start = (bf16[512,128]{1,0:T(8,128)(2,1)S(1)}, bf16[512,128]{1,0:T(8,128)(2,1)S(1)}, u32[]{:S(2)}, u32[]{:S(2)}) collective-permute-start(bf16[512,128]{1,0:T(8,128)(2,1)S(1)} %get-tuple-element.24), channel_id=1, source_target_pairs={{0,32},{32,64},{64,96},{96,128},{128,160},{160,192},{192,224},{224... | collective-permute-start | bytes 393224 | tf_op jit(solution)/shard_map/ppermute | solution.py:640
  4.4 7.1 %collective-permute-start.1 = (bf16[512,128]{1,0:T(8,128)(2,1)S(1)}, bf16[512,128]{1,0:T(8,128)(2,1)S(1)}, u32[]{:S(2)}, u32[]{:S(2)}) collective-permute-start(bf16[512,128]{1,0:T(8,128)(2,1)S(1)} %get-tuple-element.25), channel_id=1, source_target_pairs={{32,0},{64,32},{96,64},{128,96},{160,128},{192,160},{224,192},{0,2... | collective-permute-start | bytes 393224 | tf_op jit(solution)/shard_map/ppermute | solution.py:641

commit v6 on v5

--- a/solution.py
+++ b/solution.py
@@ -47,8 +47,7 @@
 PLACE = (0, 40, 80, 128, 168)
 DEPTH = 208
 HALO_ROWS = Z_HALO * X_DEV
-INNER_ROWS = HALO_ROWS // 2
-EDGE_AT = HALO_ROWS + INNER_ROWS
+EDGE_AT = HALO_ROWS
 EDGE_ROWS = SUBSETS * VIEWS * M_HALO
 SENT_ROWS = EDGE_AT + EDGE_ROWS
 TABLE = (16, 128)
@@ -332,16 +331,12 @@
     row_ref[...] = jnp.zeros_like(row_ref)
     for copy in copies:
         copy.wait()
-    for out_ref, z, inner, r in (
-        (up_ref, Z_DEV - Z_HALO, Z_HALO // 2, ROWS_DEV - M_HALO),
-        (down_ref, 0, 0, 0),
+    for out_ref, z, r in (
+        (up_ref, Z_DEV - Z_HALO, ROWS_DEV - M_HALO),
+        (down_ref, 0, 0),
     ):
         slices = vol_ref[z * X_DEV : (z + Z_HALO) * X_DEV, :]
-        rounded = slices.astype(jnp.bfloat16)
-        out_ref[0:HALO_ROWS, :] = rounded
-        left = slices - rounded.astype(jnp.float32)
-        at = inner * X_DEV
-        out_ref[HALO_ROWS:EDGE_AT, :] = left[at : at + INNER_ROWS].astype(jnp.bfloat16)
+        out_ref[0:HALO_ROWS, :] = slices.astype(jnp.bfloat16)
         for v in range(VIEWS):
             at = (v * ROWS_DEV + r) * SUBSETS
             row_ref[:, 0:COLS_DEV] = meas_ref[at : at + SUBSETS * M_HALO, :]
@@ -402,14 +397,9 @@
     def read(z, x):
         if z >= 2 * Z_HALO:
             return jnp.full((8, NY), 1.0 if z == ONES - Z_DEV else 0.0, jnp.float32)
-        sent_ref, inner = (low_ref, Z_HALO // 2) if z < Z_HALO else (high_ref, 0)
-        z = z % Z_HALO
-        at = z * X_DEV + x
-        rows = sent_ref[at : at + 8, :].astype(jnp.float32)
-        if inner <= z < inner + Z_HALO // 2:
-            at = at + HALO_ROWS - inner * X_DEV
-            rows = rows + sent_ref[at : at + 8, :].astype(jnp.float32)
-        return rows
+        sent_ref = low_ref if z < Z_HALO else high_ref
+        at = z % Z_HALO * X_DEV + x
+        return sent_ref[at : at + 8, :].astype(jnp.float32)
 
     relay(read, side_ref, True)
     for s, m_ref in ((0, m0_ref), (1, m1_ref)):

time: 69 us -> 68.5 us (level)
  transfers between devices with their start and end apart: 2 -> 2, of which waited for: 1 -> 0; matrix products, arithmetic and copies ran while one was open for 0% -> 0% of each run, Pallas kernels for 4% -> 4%
where the time goes in v6:
time: 68.5 us; the launch traced here: 68.2 us
  blocking collectives  49.8 us (73%)
  Pallas kernels  11.2 us (16%)
  starting transfers between devices  6.56 us (10%)
  between operations  0.69 us (1%)
    all_to_all x4, blocking collectives, exchanged(): lax.all_to_all(parts.reshape(shape), 'xy', split_axis=0, concat_axis=0, t...  49.8 us
    pallas_call x5, Pallas kernels, call(): pl.pallas_call(kernel, in_specs=[spec(x) for x in inputs], out_specs=[spe...  7.17 us
    ppermute x1, starting transfers between devices, local(): high = lax.ppermute(down, 'gz', [(j, i) for i, j in next_up])  4.03 us
    pallas_call x1, Pallas kernels, local(): pl.pallas_call(prepare_kernel, in_specs=[pl.BlockSpec(memory_space=vmem)]...  2.84 us
    ppermute x1, starting transfers between devices, local(): low = lax.ppermute(up, 'gz', next_up)  2.53 us
  transfers between devices with their start and end apart: 2, of which 0 were waited for; matrix products, arithmetic and copies ran while one was open for 0% of the time, Pallas kernels for 4%

profile of v6, /device:TPU:1, one launch (start us, length us, event | category | flops | bytes accessed | tf_op | source)
XLA Modules:
  0.0 68.2 jit_solution(11332248797888166818)
XLA Ops:
  0.6 1.2 %pack.1 = (bf16[368,128]{1,0:T(8,128)(2,1)S(1)}, bf16[368,128]{1,0:T(8,128)(2,1)S(1)}, f32[768,128]{1,0:T(8,128)S(1)}, f32[200,48]{1,0:T(8,128)S(1)}, s32[1,48]{1,0:T(1,128)S(1)}) custom-call(f32[768,128]{1,0:T(8,128)} %bitcast.17, f32[200,48]{1,0:T(8,128)} %bitcast.18, s32[1,48]{1,0:T(1,128)} %bitcast.19), custom_call_target="tpu_custom_call" | custom-call | tf_op jit(solution)/shard_map/pack/pallas_call | solution.py:618
  1.8 2.5 %collective-permute-start = (bf16[368,128]{1,0:T(8,128)(2,1)S(1)}, bf16[368,128]{1,0:T(8,128)(2,1)S(1)}, u32[]{:S(2)}, u32[]{:S(2)}) collective-permute-start(bf16[368,128]{1,0:T(8,128)(2,1)S(1)} %get-tuple-element.24), channel_id=1, source_target_pairs={{0,32},{32,64},{64,96},{96,128},{128,160},{160,192},{192,224},{224... | collective-permute-start | bytes 282632 | tf_op jit(solution)/shard_map/ppermute | solution.py:630
  4.4 4.0 %collective-permute-start.1 = (bf16[368,128]{1,0:T(8,128)(2,1)S(1)}, bf16[368,128]{1,0:T(8,128)(2,1)S(1)}, u32[]{:S(2)}, u32[]{:S(2)}) collective-permute-start(bf16[368,128]{1,0:T(8,128)(2,1)S(1)} %get-tuple-element.25), channel_id=1, source_target_pairs={{32,0},{64,32},{96,64},{128,96},{160,128},{192,160},{224,192},{0,2... | collective-permute-start | bytes 282632 | tf_op jit(solution)/shard_map/ppermute | solution.py:631
  8.4 2.8 %prepare.1 = (bf16[24,208,256]{2,1,0:T(8,128)(2,1)S(1)}, bf16[24,208,256]{2,1,0:T(8,128)(2,1)S(1)}, f32[24,16,256]{2,1,0:T(8,128)S(1)}, f32[2,5,24,128]{3,2,1,0:T(8,128)S(1)}, s32[16,128]{1,0:T(8,128)S(4)}) custom-call(s32[1,48]{1,0:T(1,128)S(1)} %get-tuple-element.17.order_ref, f32[768,128]{1,0:T(8,128)S(1)} %get-tuple-element.18.vol_ref, ...), custom_call_target="tpu_custom_call" | custom-call | tf_op jit(solution)/shard_map/prepare/pallas_call | solution.py:632
  11.2 0.0 collective-permute-done.low_ref
  11.2 0.0 collective-permute-done.1.high_ref
  11.3 1.8 %first.1 = (f32[384,128]{1,0:T(8,128)S(1)}, f32[24,16,256]{2,1,0:T(8,128)S(1)}, f32[5,64,128]{2,1,0:T(8,128)S(1)}) custom-call(s32[16,128]{1,0:T(8,128)S(4)} %get-tuple-element.20.table_ref, bf16[24,208,256]{2,1,0:T(8,128)(2,1)S(1)} %get-tuple-element.21.w_ref.w0_ref, f32[24,16,256]{2,1,0:T(8,128)S(1)} %get-tuple-element.22.own_ref, ...), custom_call_target="tpu_custom_call" | custom-call | tf_op jit(solution)/shard_map/first/pallas_call | solution.py:584
  13.0 16.1 %all_to_all.20 = f32[32,3,4,128]{3,2,1,0:T(4,128)S(1)} all-to-all(f32[32,3,4,128]{3,2,1,0:T(4,128)S(1)} %bitcast.15), channel_id=1, replica_groups=mesh['gz'=8,'xy'=32] {'xy'}, dimensions={0} | all-to-all | bytes 393216 | tf_op jit(solution)/shard_map/all_to_all | solution.py:596
  29.2 0.6 owner_a.1
  29.7 10.9 %all_to_all.21.recv_ref = bf16[32,8,128]{2,1,0:T(8,128)(2,1)S(1)} all-to-all(bf16[32,8,128]{2,1,0:T(8,128)(2,1)S(1)} %owner_a.1), channel_id=1, replica_groups=mesh['gz'=8,'xy'=32] {'xy'}, dimensions={0} | all-to-all | bytes 131072 | tf_op jit(solution)/shard_map/all_to_all | solution.py:596
  40.6 2.2 %middle.1 = (f32[320,128]{1,0:T(8,128)S(1)}, f32[24,16,256]{2,1,0:T(8,128)S(1)}) custom-call(s32[16,128]{1,0:T(8,128)S(4)} %get-tuple-element.20.table_ref, bf16[32,8,128]{2,1,0:T(8,128)(2,1)S(1)} %all_to_all.21.recv_ref, f32[24,16,256]{2,1,0:T(8,128)S(1)} %get-tuple-element.22.own_ref, f32[24,16,256]{2,1,0:T(8,128)S(1)} %get-tuple-element.27.side_ref, ...), custom_call_target="tpu_custom_call" | custom-call | tf_op jit(solution)/shard_map/middle/pallas_call | solution.py:584
  42.8 11.5 %all_to_all.22 = f32[32,5,2,128]{3,2,1,0:T(2,128)S(1)} all-to-all(f32[32,5,2,128]{3,2,1,0:T(2,128)S(1)} %bitcast.16), channel_id=1, replica_groups=mesh['gz'=8,'xy'=32] {'xy'}, dimensions={0} | all-to-all | bytes 327680 | tf_op jit(solution)/shard_map/all_to_all | solution.py:596
  54.3 0.5 owner_b.1
  54.8 11.3 %all_to_all.23 = f32[32,8,128]{2,1,0:T(8,128)S(1)} all-to-all(f32[32,8,128]{2,1,0:T(8,128)S(1)} %bitcast.14), channel_id=1, replica_groups=mesh['gz'=8,'xy'=32] {'xy'}, dimensions={0} | all-to-all | bytes 262144 | tf_op jit(solution)/shard_map/all_to_all | solution.py:596
  66.1 2.2 %last.1 = (f32[16,48,128]{2,1,0:T(8,128)}, f32[5,20,48]{2,1,0:T(8,128)}) custom-call(s32[16,128]{1,0:T(8,128)S(4)} %get-tuple-element.20.table_ref, f32[256,128]{1,0:T(8,128)S(1)} %bitcast.13, f32[24,16,256]{2,1,0:T(8,128)S(1)} %get-tuple-element.31.old_ref, bf16[24,208,256]{2,1,0:T(8,128)(2,1)S(1)} %get-tuple-element.29.w1_ref.w_ref), custom_call_target="tpu_custom_call" | custom-call | tf_op jit(solution)/shard_map/last/pallas_call | solution.py:584
Async XLA Ops:
  1.8 9.4 %collective-permute-start = (bf16[368,128]{1,0:T(8,128)(2,1)S(1)}, bf16[368,128]{1,0:T(8,128)(2,1)S(1)}, u32[]{:S(2)}, u32[]{:S(2)}) collective-permute-start(bf16[368,128]{1,0:T(8,128)(2,1)S(1)} %get-tuple-element.24), channel_id=1, source_target_pairs={{0,32},{32,64},{64,96},{96,128},{128,160},{160,192},{192,224},{224... | collective-permute-start | bytes 282632 | tf_op jit(solution)/shard_map/ppermute | solution.py:630
  4.4 6.9 %collective-permute-start.1 = (bf16[368,128]{1,0:T(8,128)(2,1)S(1)}, bf16[368,128]{1,0:T(8,128)(2,1)S(1)}, u32[]{:S(2)}, u32[]{:S(2)}) collective-permute-start(bf16[368,128]{1,0:T(8,128)(2,1)S(1)} %get-tuple-element.25), channel_id=1, source_target_pairs={{32,0},{64,32},{96,64},{128,96},{160,128},{192,160},{224,192},{0,2... | collective-permute-start | bytes 282632 | tf_op jit(solution)/shard_map/ppermute | solution.py:631

commit v7 on v6

--- a/solution.py
+++ b/solution.py
@@ -319,10 +319,13 @@
 
 
 def pack_kernel(
-    vol_hbm, meas_hbm, order_hbm, up_ref, down_ref, vol_ref, meas_ref, order_ref, row_ref, sems
+    vol_hbm, meas_hbm, order_hbm, up_ref, down_ref, meas_ref, order_ref, row_ref, edge_ref, sems
 ):
     copies = [
-        pltpu.make_async_copy(vol_hbm, vol_ref, sems.at[0]),
+        pltpu.make_async_copy(
+            vol_hbm.at[pl.ds((Z_DEV - Z_HALO) * X_DEV, HALO_ROWS)], edge_ref.at[0], sems.at[0]
+        ),
+        pltpu.make_async_copy(vol_hbm.at[pl.ds(0, HALO_ROWS)], edge_ref.at[1], sems.at[3]),
         pltpu.make_async_copy(meas_hbm, meas_ref, sems.at[1]),
         pltpu.make_async_copy(order_hbm, order_ref, sems.at[2]),
     ]
@@ -331,12 +334,8 @@
     row_ref[...] = jnp.zeros_like(row_ref)
     for copy in copies:
         copy.wait()
-    for out_ref, z, r in (
-        (up_ref, Z_DEV - Z_HALO, ROWS_DEV - M_HALO),
-        (down_ref, 0, 0),
-    ):
-        slices = vol_ref[z * X_DEV : (z + Z_HALO) * X_DEV, :]
-        out_ref[0:HALO_ROWS, :] = slices.astype(jnp.bfloat16)
+    for side, (out_ref, r) in enumerate(((up_ref, ROWS_DEV - M_HALO), (down_ref, 0))):
+        out_ref[0:HALO_ROWS, :] = edge_ref[side].astype(jnp.bfloat16)
         for v in range(VIEWS):
             at = (v * ROWS_DEV + r) * SUBSETS
             row_ref[:, 0:COLS_DEV] = meas_ref[at : at + SUBSETS * M_HALO, :]
@@ -349,10 +348,12 @@
 
 
 def prepare_kernel(
-    order_ref, vol_ref, meas_ref,
-    w0_ref, w1_ref, own_ref, mown_ref, table_ref, u_ref, flat_ref, sem,
+    order_ref, meas_ref, vol_hbm,
+    w0_ref, w1_ref, own_ref, mown_ref, table_ref, u_ref, flat_ref, vol_ref, sem, vol_sem,
 ):
     xy = lax.axis_index("xy")
+    volume = pltpu.make_async_copy(vol_hbm, vol_ref, vol_sem)
+    volume.start()
     chosen = iota((TABLE[0], ANGLES), 0) == iota((TABLE[0], ANGLES), 1)
     chosen = jnp.where(chosen, order_ref[...].astype(jnp.float32), 0.0)
     chosen = jnp.broadcast_to(jnp.sum(chosen, axis=1, keepdims=True), TABLE)
@@ -362,9 +363,6 @@
     flat_ref[...], own = fill_table(cosine, sine, xy)
     copy = pltpu.make_async_copy(flat_ref, table_ref, sem)
     copy.start()
-    relay(
-        lambda z, x: vol_ref[pl.ds(pl.multiple_of(z * X_DEV + x, 8), 8), :], own_ref, False
-    )
     mown_ref[...] = jnp.zeros_like(mown_ref)
     for s in range(SUBSETS):
         for v in range(VIEWS):
@@ -382,6 +380,10 @@
             return nothing
 
         lax.fori_loop(0, TILES // 8, step, 0)
+    volume.wait()
+    relay(
+        lambda z, x: vol_ref[pl.ds(pl.multiple_of(z * X_DEV + x, 8), 8), :], own_ref, False
+    )
 
 
 def first_kernel(
@@ -615,14 +617,16 @@
 
     sent = vmem((SENT_ROWS, 128), bf16)
     hbm = pl.BlockSpec(memory_space=pltpu.HBM)
-    up, down, flat, rows, order = pl.pallas_call(
+    up, down, rows, order = pl.pallas_call(
         pack_kernel,
         in_specs=[hbm] * 3,
-        out_specs=[pl.BlockSpec(memory_space=vmem)] * 5,
-        out_shape=[
-            sent, sent, vmem(flat.shape, f32), vmem(rows.shape, f32), vmem((1, ANGLES), jnp.int32)
+        out_specs=[pl.BlockSpec(memory_space=vmem)] * 4,
+        out_shape=[sent, sent, vmem(rows.shape, f32), vmem((1, ANGLES), jnp.int32)],
+        scratch_shapes=[
+            vmem((SUBSETS * M_HALO, 128), f32),
+            vmem((2, HALO_ROWS, NY), f32),
+            pltpu.SemaphoreType.DMA((4,)),
         ],
-        scratch_shapes=[vmem((SUBSETS * M_HALO, 128), f32), pltpu.SemaphoreType.DMA((3,))],
         compiler_params=pltpu.CompilerParams(vmem_limit_bytes=12 * 1024 * 1024),
         name="pack",
     )(*(pltpu.with_memory_space_constraint(x, pltpu.HBM) for x in (flat, rows, order)))
@@ -631,17 +635,24 @@
     high = lax.ppermute(down, "gz", [(j, i) for i, j in next_up])
     w0, w1, own, mown, table = pl.pallas_call(
         prepare_kernel,
-        in_specs=[pl.BlockSpec(memory_space=vmem)] * 3,
+        in_specs=[pl.BlockSpec(memory_space=vmem)] * 2 + [hbm],
         out_specs=[pl.BlockSpec(memory_space=m) for m in (vmem, vmem, vmem, vmem, pltpu.SMEM)],
         out_shape=[
             made, made, slices, vmem((SUBSETS, VIEWS, 24, 128), f32), pltpu.SMEM(TABLE, jnp.int32)
         ],
         scratch_shapes=[
-            vmem((VIEWS, TILES, VOXELS), f32), vmem(TABLE, jnp.int32), pltpu.SemaphoreType.DMA
+            vmem((VIEWS, TILES, VOXELS), f32),
+            vmem(TABLE, jnp.int32),
+            vmem((Z_DEV * X_DEV, NY), f32),
+            pltpu.SemaphoreType.DMA,
+            pltpu.SemaphoreType.DMA,
         ],
         compiler_params=pltpu.CompilerParams(vmem_limit_bytes=12 * 1024 * 1024),
         name="prepare",
-    )(*(pltpu.with_memory_space_constraint(x, vmem) for x in (order, flat, rows)))
+    )(
+        *(pltpu.with_memory_space_constraint(x, vmem) for x in (order, rows)),
+        pltpu.with_memory_space_constraint(flat, pltpu.HBM),
+    )
     partial, side, m1 = call(
         first_kernel,
         (table, w0, own, mown, low, high),

time: 68.5 us -> 69.1 us (level)
  transfers between devices with their start and end apart: 2 -> 2, of which waited for: 0 -> 0; matrix products, arithmetic and copies ran while one was open for 0% -> 0% of each run, Pallas kernels for 4% -> 5%
where the time goes in v7:
time: 69.1 us; the launch traced here: 68.8 us
  blocking collectives  49.8 us (72%)
  Pallas kernels  11.8 us (17%)
  starting transfers between devices  6.56 us (9%)
    all_to_all x4, blocking collectives, exchanged(): lax.all_to_all(parts.reshape(shape), 'xy', split_axis=0, concat_axis=0, t...  49.8 us
    pallas_call x5, Pallas kernels, call(): pl.pallas_call(kernel, in_specs=[spec(x) for x in inputs], out_specs=[spe...  7.16 us
    ppermute x1, starting transfers between devices, local(): high = lax.ppermute(down, 'gz', [(j, i) for i, j in next_up])  4.03 us
    pallas_call x1, Pallas kernels, local(): pl.pallas_call(prepare_kernel, in_specs=[pl.BlockSpec(memory_space=vmem)]...  3.41 us
    ppermute x1, starting transfers between devices, local(): low = lax.ppermute(up, 'gz', next_up)  2.53 us
  transfers between devices with their start and end apart: 2, of which 0 were waited for; matrix products, arithmetic and copies ran while one was open for 0% of the time, Pallas kernels for 5%

profile of v7, /device:TPU:1, one launch (start us, length us, event | category | flops | bytes accessed | tf_op | source)
XLA Modules:
  0.0 68.8 jit_solution(17717620632007934162)
XLA Ops:
  0.6 1.2 %pack.1 = (bf16[368,128]{1,0:T(8,128)(2,1)S(1)}, bf16[368,128]{1,0:T(8,128)(2,1)S(1)}, f32[200,48]{1,0:T(8,128)S(1)}, s32[1,48]{1,0:T(1,128)S(1)}) custom-call(f32[768,128]{1,0:T(8,128)} %bitcast.17, f32[200,48]{1,0:T(8,128)} %bitcast.19, s32[1,48]{1,0:T(1,128)} %bitcast.20), custom_call_target="tpu_custom_call" | custom-call | tf_op jit(solution)/shard_map/pack/pallas_call | solution.py:620
  1.9 2.5 %collective-permute-start = (bf16[368,128]{1,0:T(8,128)(2,1)S(1)}, bf16[368,128]{1,0:T(8,128)(2,1)S(1)}, u32[]{:S(2)}, u32[]{:S(2)}) collective-permute-start(bf16[368,128]{1,0:T(8,128)(2,1)S(1)} %get-tuple-element.22), channel_id=1, source_target_pairs={{0,32},{32,64},{64,96},{96,128},{128,160},{160,192},{192,224},{224... | collective-permute-start | bytes 282632 | tf_op jit(solution)/shard_map/ppermute | solution.py:634
  4.4 4.0 %collective-permute-start.1 = (bf16[368,128]{1,0:T(8,128)(2,1)S(1)}, bf16[368,128]{1,0:T(8,128)(2,1)S(1)}, u32[]{:S(2)}, u32[]{:S(2)}) collective-permute-start(bf16[368,128]{1,0:T(8,128)(2,1)S(1)} %get-tuple-element.23), channel_id=1, source_target_pairs={{32,0},{64,32},{96,64},{128,96},{160,128},{192,160},{224,192},{0,2... | collective-permute-start | bytes 282632 | tf_op jit(solution)/shard_map/ppermute | solution.py:635
  8.4 3.4 %prepare.1 = (bf16[24,208,256]{2,1,0:T(8,128)(2,1)S(1)}, bf16[24,208,256]{2,1,0:T(8,128)(2,1)S(1)}, f32[24,16,256]{2,1,0:T(8,128)S(1)}, f32[2,5,24,128]{3,2,1,0:T(8,128)S(1)}, s32[16,128]{1,0:T(8,128)S(4)}) custom-call(s32[1,48]{1,0:T(1,128)S(1)} %get-tuple-element.16.order_ref, f32[200,48]{1,0:T(8,128)S(1)} %get-tuple-element.17.meas_ref, f32[768,128]{1,0:T(8,128)} %bitcast.18), custom_call_target="tpu_custom_call" | custom-call | tf_op jit(solution)/shard_map/prepare/pallas_call | solution.py:636
  11.8 0.0 collective-permute-done.low_ref
  11.9 0.0 collective-permute-done.1.high_ref
  11.9 1.8 %first.1 = (f32[384,128]{1,0:T(8,128)S(1)}, f32[24,16,256]{2,1,0:T(8,128)S(1)}, f32[5,64,128]{2,1,0:T(8,128)S(1)}) custom-call(s32[16,128]{1,0:T(8,128)S(4)} %get-tuple-element.18.table_ref, bf16[24,208,256]{2,1,0:T(8,128)(2,1)S(1)} %get-tuple-element.19.w_ref.w0_ref, f32[24,16,256]{2,1,0:T(8,128)S(1)} %get-tuple-element.20.own_ref, ...), custom_call_target="tpu_custom_call" | custom-call | tf_op jit(solution)/shard_map/first/pallas_call | solution.py:586
  13.6 16.1 %all_to_all.20 = f32[32,3,4,128]{3,2,1,0:T(4,128)S(1)} all-to-all(f32[32,3,4,128]{3,2,1,0:T(4,128)S(1)} %bitcast.15), channel_id=1, replica_groups=mesh['gz'=8,'xy'=32] {'xy'}, dimensions={0} | all-to-all | bytes 393216 | tf_op jit(solution)/shard_map/all_to_all | solution.py:598
  29.8 0.6 owner_a.1
  30.3 10.9 %all_to_all.21.recv_ref = bf16[32,8,128]{2,1,0:T(8,128)(2,1)S(1)} all-to-all(bf16[32,8,128]{2,1,0:T(8,128)(2,1)S(1)} %owner_a.1), channel_id=1, replica_groups=mesh['gz'=8,'xy'=32] {'xy'}, dimensions={0} | all-to-all | bytes 131072 | tf_op jit(solution)/shard_map/all_to_all | solution.py:598
  41.2 2.2 %middle.1 = (f32[320,128]{1,0:T(8,128)S(1)}, f32[24,16,256]{2,1,0:T(8,128)S(1)}) custom-call(s32[16,128]{1,0:T(8,128)S(4)} %get-tuple-element.18.table_ref, bf16[32,8,128]{2,1,0:T(8,128)(2,1)S(1)} %all_to_all.21.recv_ref, f32[24,16,256]{2,1,0:T(8,128)S(1)} %get-tuple-element.20.own_ref, f32[24,16,256]{2,1,0:T(8,128)S(1)} %get-tuple-element.25.side_ref, ...), custom_call_target="tpu_custom_call" | custom-call | tf_op jit(solution)/shard_map/middle/pallas_call | solution.py:586
  43.4 11.5 %all_to_all.22 = f32[32,5,2,128]{3,2,1,0:T(2,128)S(1)} all-to-all(f32[32,5,2,128]{3,2,1,0:T(2,128)S(1)} %bitcast.16), channel_id=1, replica_groups=mesh['gz'=8,'xy'=32] {'xy'}, dimensions={0} | all-to-all | bytes 327680 | tf_op jit(solution)/shard_map/all_to_all | solution.py:598
  54.9 0.5 owner_b.1
  55.4 11.2 %all_to_all.23 = f32[32,8,128]{2,1,0:T(8,128)S(1)} all-to-all(f32[32,8,128]{2,1,0:T(8,128)S(1)} %bitcast.14), channel_id=1, replica_groups=mesh['gz'=8,'xy'=32] {'xy'}, dimensions={0} | all-to-all | bytes 262144 | tf_op jit(solution)/shard_map/all_to_all | solution.py:598
  66.6 2.2 %last.1 = (f32[16,48,128]{2,1,0:T(8,128)}, f32[5,20,48]{2,1,0:T(8,128)}) custom-call(s32[16,128]{1,0:T(8,128)S(4)} %get-tuple-element.18.table_ref, f32[256,128]{1,0:T(8,128)S(1)} %bitcast.13, f32[24,16,256]{2,1,0:T(8,128)S(1)} %get-tuple-element.29.old_ref, bf16[24,208,256]{2,1,0:T(8,128)(2,1)S(1)} %get-tuple-element.27.w1_ref.w_ref), custom_call_target="tpu_custom_call" | custom-call | tf_op jit(solution)/shard_map/last/pallas_call | solution.py:586
Async XLA Ops:
  1.9 10.0 %collective-permute-start = (bf16[368,128]{1,0:T(8,128)(2,1)S(1)}, bf16[368,128]{1,0:T(8,128)(2,1)S(1)}, u32[]{:S(2)}, u32[]{:S(2)}) collective-permute-start(bf16[368,128]{1,0:T(8,128)(2,1)S(1)} %get-tuple-element.22), channel_id=1, source_target_pairs={{0,32},{32,64},{64,96},{96,128},{128,160},{160,192},{192,224},{224... | collective-permute-start | bytes 282632 | tf_op jit(solution)/shard_map/ppermute | solution.py:634
  4.4 7.5 %collective-permute-start.1 = (bf16[368,128]{1,0:T(8,128)(2,1)S(1)}, bf16[368,128]{1,0:T(8,128)(2,1)S(1)}, u32[]{:S(2)}, u32[]{:S(2)}) collective-permute-start(bf16[368,128]{1,0:T(8,128)(2,1)S(1)} %get-tuple-element.23), channel_id=1, source_target_pairs={{32,0},{64,32},{96,64},{128,96},{160,128},{192,160},{224,192},{0,2... | collective-permute-start | bytes 282632 | tf_op jit(solution)/shard_map/ppermute | solution.py:635

commit v8 on v6

--- a/solution.py
+++ b/solution.py
@@ -146,7 +146,7 @@
         offsets = tile_offsets(table_ref, subset, tile)
         part = lax.dot_general(
             w_ref[tile],
-            jnp.concatenate([slices(tile)] * 4, axis=0),
+            jnp.concatenate([slices(tile)] * 3, axis=0),
             (((1,), (1,)), ((), ())),
             preferred_element_type=jnp.float32,
         )
@@ -155,8 +155,8 @@
     per = ROWS_PER[subset]
     half = per + 1
     size = GROUPS * 2 * half
-    k = iota((size, 128), 0)
-    lane = iota((size, 128), 1)
+    k = iota((size, 3 * Z_PAD), 0)
+    lane = iota((size, 3 * Z_PAD), 1)
     i = lane & (Z_PAD - 1)
     group = (k * 43) >> 9 if half == 6 else (k * 205) >> 11
     slot = k - group * 2 * half
@@ -166,7 +166,10 @@
     rows = jnp.where((slot == per) & (i == ONES), 1.0, rows)
     rounded = rows.astype(jnp.bfloat16).astype(jnp.float32)
     rows = jnp.where(lane < 2 * Z_PAD, rounded, rows - rounded).astype(jnp.bfloat16)
-    left_over = (iota((WIN, 128), 1) & Z_PAD) != 0
+    left_over = (iota((WIN, 3 * Z_PAD), 1) & Z_PAD) != 0
+    k = iota((size, 128), 0)
+    group = (k * 43) >> 9 if half == 6 else (k * 205) >> 11
+    is_low = k - group * 2 * half < half
     used = GROUPS * VIEWS * 2 * half
     out_ref[used:, :] = jnp.zeros((out_ref.shape[0] - used, 128), jnp.float32)
     for v in range(VIEWS):
@@ -609,7 +612,7 @@
     made = vmem((TILES, DEPTH, VOXELS), bf16)
     slices = vmem((TILES, Z_DEV, VOXELS), f32)
     sm_scratch = vmem((VIEWS, Z_PAD, LANES), f32)
-    acc_scratch = [vmem((WIN, 128), f32)] * VIEWS
+    acc_scratch = [vmem((WIN, 3 * Z_PAD), f32)] * VIEWS
     row_scratch = vmem((8, FULL), f32)
     owner_scratch = [row_scratch] * (2 + SUMS)
 

time: 68.5 us -> 68.5 us (level)
  no operation moved by 1% of the time
where the time goes in v8:
time: 68.5 us; the launch traced here: 68.2 us
  blocking collectives  49.8 us (73%)
  Pallas kernels  11.2 us (16%)
  starting transfers between devices  6.56 us (10%)
  between operations  0.69 us (1%)
    all_to_all x4, blocking collectives, exchanged(): lax.all_to_all(parts.reshape(shape), 'xy', split_axis=0, concat_axis=0, t...  49.8 us
    pallas_call x5, Pallas kernels, call(): pl.pallas_call(kernel, in_specs=[spec(x) for x in inputs], out_specs=[spe...  7.18 us
    ppermute x1, starting transfers between devices, local(): high = lax.ppermute(down, 'gz', [(j, i) for i, j in next_up])  4.03 us
    pallas_call x1, Pallas kernels, local(): pl.pallas_call(prepare_kernel, in_specs=[pl.BlockSpec(memory_space=vmem)]...  2.84 us
    ppermute x1, starting transfers between devices, local(): low = lax.ppermute(up, 'gz', next_up)  2.53 us
  transfers between devices with their start and end apart: 2, of which 0 were waited for; matrix products, arithmetic and copies ran while one was open for 0% of the time, Pallas kernels for 4%

profile of v8, /device:TPU:1, one launch (start us, length us, event | category | flops | bytes accessed | tf_op | source)
XLA Modules:
  0.0 68.2 jit_solution(1545449166774961087)
XLA Ops:
  0.6 1.2 %pack.1 = (bf16[368,128]{1,0:T(8,128)(2,1)S(1)}, bf16[368,128]{1,0:T(8,128)(2,1)S(1)}, f32[768,128]{1,0:T(8,128)S(1)}, f32[200,48]{1,0:T(8,128)S(1)}, s32[1,48]{1,0:T(1,128)S(1)}) custom-call(f32[768,128]{1,0:T(8,128)} %bitcast.17, f32[200,48]{1,0:T(8,128)} %bitcast.18, s32[1,48]{1,0:T(1,128)} %bitcast.19), custom_call_target="tpu_custom_call" | custom-call | tf_op jit(solution)/shard_map/pack/pallas_call | solution.py:621
  1.8 2.5 %collective-permute-start = (bf16[368,128]{1,0:T(8,128)(2,1)S(1)}, bf16[368,128]{1,0:T(8,128)(2,1)S(1)}, u32[]{:S(2)}, u32[]{:S(2)}) collective-permute-start(bf16[368,128]{1,0:T(8,128)(2,1)S(1)} %get-tuple-element.24), channel_id=1, source_target_pairs={{0,32},{32,64},{64,96},{96,128},{128,160},{160,192},{192,224},{224... | collective-permute-start | bytes 282632 | tf_op jit(solution)/shard_map/ppermute | solution.py:633
  4.4 4.0 %collective-permute-start.1 = (bf16[368,128]{1,0:T(8,128)(2,1)S(1)}, bf16[368,128]{1,0:T(8,128)(2,1)S(1)}, u32[]{:S(2)}, u32[]{:S(2)}) collective-permute-start(bf16[368,128]{1,0:T(8,128)(2,1)S(1)} %get-tuple-element.25), channel_id=1, source_target_pairs={{32,0},{64,32},{96,64},{128,96},{160,128},{192,160},{224,192},{0,2... | collective-permute-start | bytes 282632 | tf_op jit(solution)/shard_map/ppermute | solution.py:634
  8.4 2.8 %prepare.1 = (bf16[24,208,256]{2,1,0:T(8,128)(2,1)S(1)}, bf16[24,208,256]{2,1,0:T(8,128)(2,1)S(1)}, f32[24,16,256]{2,1,0:T(8,128)S(1)}, f32[2,5,24,128]{3,2,1,0:T(8,128)S(1)}, s32[16,128]{1,0:T(8,128)S(4)}) custom-call(s32[1,48]{1,0:T(1,128)S(1)} %get-tuple-element.17.order_ref, f32[768,128]{1,0:T(8,128)S(1)} %get-tuple-element.18.vol_ref, ...), custom_call_target="tpu_custom_call" | custom-call | tf_op jit(solution)/shard_map/prepare/pallas_call | solution.py:635
  11.2 0.0 collective-permute-done.low_ref
  11.2 0.0 collective-permute-done.1.high_ref
  11.3 1.8 %first.1 = (f32[384,128]{1,0:T(8,128)S(1)}, f32[24,16,256]{2,1,0:T(8,128)S(1)}, f32[5,64,128]{2,1,0:T(8,128)S(1)}) custom-call(s32[16,128]{1,0:T(8,128)S(4)} %get-tuple-element.20.table_ref, bf16[24,208,256]{2,1,0:T(8,128)(2,1)S(1)} %get-tuple-element.21.w_ref.w0_ref, f32[24,16,256]{2,1,0:T(8,128)S(1)} %get-tuple-element.22.own_ref, ...), custom_call_target="tpu_custom_call" | custom-call | tf_op jit(solution)/shard_map/first/pallas_call | solution.py:587
  13.1 16.1 %all_to_all.20 = f32[32,3,4,128]{3,2,1,0:T(4,128)S(1)} all-to-all(f32[32,3,4,128]{3,2,1,0:T(4,128)S(1)} %bitcast.15), channel_id=1, replica_groups=mesh['gz'=8,'xy'=32] {'xy'}, dimensions={0} | all-to-all | bytes 393216 | tf_op jit(solution)/shard_map/all_to_all | solution.py:599
  29.2 0.6 owner_a.1
  29.8 10.9 %all_to_all.21.recv_ref = bf16[32,8,128]{2,1,0:T(8,128)(2,1)S(1)} all-to-all(bf16[32,8,128]{2,1,0:T(8,128)(2,1)S(1)} %owner_a.1), channel_id=1, replica_groups=mesh['gz'=8,'xy'=32] {'xy'}, dimensions={0} | all-to-all | bytes 131072 | tf_op jit(solution)/shard_map/all_to_all | solution.py:599
  40.7 2.2 %middle.1 = (f32[320,128]{1,0:T(8,128)S(1)}, f32[24,16,256]{2,1,0:T(8,128)S(1)}) custom-call(s32[16,128]{1,0:T(8,128)S(4)} %get-tuple-element.20.table_ref, bf16[32,8,128]{2,1,0:T(8,128)(2,1)S(1)} %all_to_all.21.recv_ref, f32[24,16,256]{2,1,0:T(8,128)S(1)} %get-tuple-element.22.own_ref, f32[24,16,256]{2,1,0:T(8,128)S(1)} %get-tuple-element.27.side_ref, ...), custom_call_target="tpu_custom_call" | custom-call | tf_op jit(solution)/shard_map/middle/pallas_call | solution.py:587
  42.8 11.5 %all_to_all.22 = f32[32,5,2,128]{3,2,1,0:T(2,128)S(1)} all-to-all(f32[32,5,2,128]{3,2,1,0:T(2,128)S(1)} %bitcast.16), channel_id=1, replica_groups=mesh['gz'=8,'xy'=32] {'xy'}, dimensions={0} | all-to-all | bytes 327680 | tf_op jit(solution)/shard_map/all_to_all | solution.py:599
  54.3 0.5 owner_b.1
  54.8 11.2 %all_to_all.23 = f32[32,8,128]{2,1,0:T(8,128)S(1)} all-to-all(f32[32,8,128]{2,1,0:T(8,128)S(1)} %bitcast.14), channel_id=1, replica_groups=mesh['gz'=8,'xy'=32] {'xy'}, dimensions={0} | all-to-all | bytes 262144 | tf_op jit(solution)/shard_map/all_to_all | solution.py:599
  66.1 2.2 %last.1 = (f32[16,48,128]{2,1,0:T(8,128)}, f32[5,20,48]{2,1,0:T(8,128)}) custom-call(s32[16,128]{1,0:T(8,128)S(4)} %get-tuple-element.20.table_ref, f32[256,128]{1,0:T(8,128)S(1)} %bitcast.13, f32[24,16,256]{2,1,0:T(8,128)S(1)} %get-tuple-element.31.old_ref, bf16[24,208,256]{2,1,0:T(8,128)(2,1)S(1)} %get-tuple-element.29.w1_ref.w_ref), custom_call_target="tpu_custom_call" | custom-call | tf_op jit(solution)/shard_map/last/pallas_call | solution.py:587
Async XLA Ops:
  1.8 9.4 %collective-permute-start = (bf16[368,128]{1,0:T(8,128)(2,1)S(1)}, bf16[368,128]{1,0:T(8,128)(2,1)S(1)}, u32[]{:S(2)}, u32[]{:S(2)}) collective-permute-start(bf16[368,128]{1,0:T(8,128)(2,1)S(1)} %get-tuple-element.24), channel_id=1, source_target_pairs={{0,32},{32,64},{64,96},{96,128},{128,160},{160,192},{192,224},{224... | collective-permute-start | bytes 282632 | tf_op jit(solution)/shard_map/ppermute | solution.py:633
  4.4 6.9 %collective-permute-start.1 = (bf16[368,128]{1,0:T(8,128)(2,1)S(1)}, bf16[368,128]{1,0:T(8,128)(2,1)S(1)}, u32[]{:S(2)}, u32[]{:S(2)}) collective-permute-start(bf16[368,128]{1,0:T(8,128)(2,1)S(1)} %get-tuple-element.25), channel_id=1, source_target_pairs={{32,0},{64,32},{96,64},{128,96},{160,128},{192,160},{224,192},{0,2... | collective-permute-start | bytes 282632 | tf_op jit(solution)/shard_map/ppermute | solution.py:634

commit v9 on v6

--- a/solution.py
+++ b/solution.py
@@ -225,7 +225,7 @@
     picked = jnp.where(k == ((j >> 2) << 3) + 4 + (j & 3), 1.0, 0.0).astype(jnp.bfloat16)
     rows = jnp.where(i >= 2 * Z_PAD, picked.astype(jnp.float32), rows.astype(jnp.float32))
     rows = rows.astype(jnp.bfloat16)
-    ones = iota((Z_PAD, LANES), 0) == ONES
+    ones = iota((Z_PAD, LANES), 0) == Z_DEV
     part = iota((GOT, 128), 0) & 7
     exact = (part >= 4) & (iota((GOT, 128), 1) >= MEAS_AT - 128)
     for v in range(VIEWS):
@@ -248,14 +248,14 @@
         res_ref[v] = own[0:ROWS_DEV, 0:COLS_DEV]
 
 
-def windows(sm_ref, offsets):
-    lane = iota((Z_PAD, 128), 1)
+def windows(sm_ref, offsets, size):
+    lane = iota((size, 128), 1)
     placed = []
     for v in range(VIEWS):
         at = PLACE[v] & 127
         shift = (at - offsets[v]) & 127
-        low = pltpu.roll(sm_ref[v, :, 0:128], shift, 1)
-        high = pltpu.roll(sm_ref[v, :, 128:256], shift, 1)
+        low = pltpu.roll(sm_ref[v, 0:size, 0:128], shift, 1)
+        high = pltpu.roll(sm_ref[v, 0:size, 128:256], shift, 1)
         placed.append(jnp.where(lane < at + 128 - offsets[v], low, high))
     first = jnp.where(lane < 40, placed[0], jnp.where(lane < 80, placed[1], placed[2]))
     first = jnp.where(lane < 120, first, 0.0)
@@ -264,17 +264,17 @@
     return both.astype(jnp.bfloat16)[:, 0:DEPTH]
 
 
-def backward(w_ref, sm_ref, table_ref, old, store, subset, gz):
-    zi = slice_of(iota((Z_PAD, LANES), 0), gz)
-    inside = iota((Z_PAD, LANES), 0) < Z_ALL
-    total = jnp.sum(jnp.where(inside, hat(iota((Z_PAD, LANES), 1), zi), 0.0), axis=1, keepdims=True)
+def backward(w_ref, sm_ref, table_ref, old, store, subset, gz, size, ones):
+    zi = slice_of(iota((size, LANES), 0), gz)
+    inside = iota((size, LANES), 0) < min(Z_ALL, ones)
+    total = jnp.sum(jnp.where(inside, hat(iota((size, LANES), 1), zi), 0.0), axis=1, keepdims=True)
 
     for tile in range(TILES):
         offsets = tile_offsets(table_ref, subset, tile)
         back = jnp.dot(
-            windows(sm_ref, offsets), w_ref[tile], preferred_element_type=jnp.float32
+            windows(sm_ref, offsets, size), w_ref[tile], preferred_element_type=jnp.float32
         )
-        norm = total * back[ONES : ONES + 1, :]
+        norm = total * back[ones : ones + 1, :]
         store(tile, old(tile), back / jnp.maximum(norm, 1.0))
 
 
@@ -446,7 +446,7 @@
         new_ref[tile] = new[0:Z_DEV]
         vb_ref[tile] = new.astype(jnp.bfloat16)
 
-    backward(w0_ref, sm_ref, table_ref, old, store, 0, gz)
+    backward(w0_ref, sm_ref, table_ref, old, store, 0, gz, Z_PAD, ONES)
     forward(w1_ref, lambda tile: vb_ref[tile], acc_refs, m_ref, table_ref, out_ref, 1, gz)
 
 
@@ -481,7 +481,7 @@
         )
         copies[-1].start()
 
-    backward(w_ref, sm_ref, table_ref, lambda tile: old_ref[tile], store, 1, gz)
+    backward(w_ref, sm_ref, table_ref, lambda tile: old_ref[tile], store, 1, gz, 24, Z_DEV)
     for copy in copies:
         copy.wait()
 

time: 68.5 us -> 68.2 us (level)
  no operation moved by 1% of the time
where the time goes in v9:
time: 68.2 us; the launch traced here: 67.9 us
  blocking collectives  49.8 us (73%)
  Pallas kernels  10.9 us (16%)
  starting transfers between devices  6.56 us (10%)
  between operations  0.69 us (1%)
    all_to_all x4, blocking collectives, exchanged(): lax.all_to_all(parts.reshape(shape), 'xy', split_axis=0, concat_axis=0, t...  49.8 us
    pallas_call x5, Pallas kernels, call(): pl.pallas_call(kernel, in_specs=[spec(x) for x in inputs], out_specs=[spe...  6.88 us
    ppermute x1, starting transfers between devices, local(): high = lax.ppermute(down, 'gz', [(j, i) for i, j in next_up])  4.03 us
    pallas_call x1, Pallas kernels, local(): pl.pallas_call(prepare_kernel, in_specs=[pl.BlockSpec(memory_space=vmem)]...  2.84 us
    ppermute x1, starting transfers between devices, local(): low = lax.ppermute(up, 'gz', next_up)  2.53 us
  transfers between devices with their start and end apart: 2, of which 0 were waited for; matrix products, arithmetic and copies ran while one was open for 0% of the time, Pallas kernels for 4%

profile of v9, /device:TPU:1, one launch (start us, length us, event | category | flops | bytes accessed | tf_op | source)
XLA Modules:
  0.0 67.9 jit_solution(7168289608874626993)
XLA Ops:
  0.6 1.2 %pack.1 = (bf16[368,128]{1,0:T(8,128)(2,1)S(1)}, bf16[368,128]{1,0:T(8,128)(2,1)S(1)}, f32[768,128]{1,0:T(8,128)S(1)}, f32[200,48]{1,0:T(8,128)S(1)}, s32[1,48]{1,0:T(1,128)S(1)}) custom-call(f32[768,128]{1,0:T(8,128)} %bitcast.17, f32[200,48]{1,0:T(8,128)} %bitcast.18, s32[1,48]{1,0:T(1,128)} %bitcast.19), custom_call_target="tpu_custom_call" | custom-call | tf_op jit(solution)/shard_map/pack/pallas_call | solution.py:618
  1.8 2.5 %collective-permute-start = (bf16[368,128]{1,0:T(8,128)(2,1)S(1)}, bf16[368,128]{1,0:T(8,128)(2,1)S(1)}, u32[]{:S(2)}, u32[]{:S(2)}) collective-permute-start(bf16[368,128]{1,0:T(8,128)(2,1)S(1)} %get-tuple-element.24), channel_id=1, source_target_pairs={{0,32},{32,64},{64,96},{96,128},{128,160},{160,192},{192,224},{224... | collective-permute-start | bytes 282632 | tf_op jit(solution)/shard_map/ppermute | solution.py:630
  4.4 4.0 %collective-permute-start.1 = (bf16[368,128]{1,0:T(8,128)(2,1)S(1)}, bf16[368,128]{1,0:T(8,128)(2,1)S(1)}, u32[]{:S(2)}, u32[]{:S(2)}) collective-permute-start(bf16[368,128]{1,0:T(8,128)(2,1)S(1)} %get-tuple-element.25), channel_id=1, source_target_pairs={{32,0},{64,32},{96,64},{128,96},{160,128},{192,160},{224,192},{0,2... | collective-permute-start | bytes 282632 | tf_op jit(solution)/shard_map/ppermute | solution.py:631
  8.4 2.8 %prepare.1 = (bf16[24,208,256]{2,1,0:T(8,128)(2,1)S(1)}, bf16[24,208,256]{2,1,0:T(8,128)(2,1)S(1)}, f32[24,16,256]{2,1,0:T(8,128)S(1)}, f32[2,5,24,128]{3,2,1,0:T(8,128)S(1)}, s32[16,128]{1,0:T(8,128)S(4)}) custom-call(s32[1,48]{1,0:T(1,128)S(1)} %get-tuple-element.17.order_ref, f32[768,128]{1,0:T(8,128)S(1)} %get-tuple-element.18.vol_ref, ...), custom_call_target="tpu_custom_call" | custom-call | tf_op jit(solution)/shard_map/prepare/pallas_call | solution.py:632
  11.2 0.0 collective-permute-done.low_ref
  11.2 0.0 collective-permute-done.1.high_ref
  11.3 1.8 %first.1 = (f32[384,128]{1,0:T(8,128)S(1)}, f32[24,16,256]{2,1,0:T(8,128)S(1)}, f32[5,64,128]{2,1,0:T(8,128)S(1)}) custom-call(s32[16,128]{1,0:T(8,128)S(4)} %get-tuple-element.20.table_ref, bf16[24,208,256]{2,1,0:T(8,128)(2,1)S(1)} %get-tuple-element.21.w_ref.w0_ref, f32[24,16,256]{2,1,0:T(8,128)S(1)} %get-tuple-element.22.own_ref, ...), custom_call_target="tpu_custom_call" | custom-call | tf_op jit(solution)/shard_map/first/pallas_call | solution.py:584
  13.0 16.1 %all_to_all.20 = f32[32,3,4,128]{3,2,1,0:T(4,128)S(1)} all-to-all(f32[32,3,4,128]{3,2,1,0:T(4,128)S(1)} %bitcast.15), channel_id=1, replica_groups=mesh['gz'=8,'xy'=32] {'xy'}, dimensions={0} | all-to-all | bytes 393216 | tf_op jit(solution)/shard_map/all_to_all | solution.py:596
  29.2 0.6 owner_a.1
  29.7 10.9 %all_to_all.21.recv_ref = bf16[32,8,128]{2,1,0:T(8,128)(2,1)S(1)} all-to-all(bf16[32,8,128]{2,1,0:T(8,128)(2,1)S(1)} %owner_a.1), channel_id=1, replica_groups=mesh['gz'=8,'xy'=32] {'xy'}, dimensions={0} | all-to-all | bytes 131072 | tf_op jit(solution)/shard_map/all_to_all | solution.py:596
  40.7 2.2 %middle.1 = (f32[320,128]{1,0:T(8,128)S(1)}, f32[24,16,256]{2,1,0:T(8,128)S(1)}) custom-call(s32[16,128]{1,0:T(8,128)S(4)} %get-tuple-element.20.table_ref, bf16[32,8,128]{2,1,0:T(8,128)(2,1)S(1)} %all_to_all.21.recv_ref, f32[24,16,256]{2,1,0:T(8,128)S(1)} %get-tuple-element.22.own_ref, f32[24,16,256]{2,1,0:T(8,128)S(1)} %get-tuple-element.27.side_ref, ...), custom_call_target="tpu_custom_call" | custom-call | tf_op jit(solution)/shard_map/middle/pallas_call | solution.py:584
  42.8 11.5 %all_to_all.22 = f32[32,5,2,128]{3,2,1,0:T(2,128)S(1)} all-to-all(f32[32,5,2,128]{3,2,1,0:T(2,128)S(1)} %bitcast.16), channel_id=1, replica_groups=mesh['gz'=8,'xy'=32] {'xy'}, dimensions={0} | all-to-all | bytes 327680 | tf_op jit(solution)/shard_map/all_to_all | solution.py:596
  54.3 0.5 owner_b.1
  54.8 11.3 %all_to_all.23 = f32[32,8,128]{2,1,0:T(8,128)S(1)} all-to-all(f32[32,8,128]{2,1,0:T(8,128)S(1)} %bitcast.14), channel_id=1, replica_groups=mesh['gz'=8,'xy'=32] {'xy'}, dimensions={0} | all-to-all | bytes 262144 | tf_op jit(solution)/shard_map/all_to_all | solution.py:596
  66.1 1.9 %last.1 = (f32[16,48,128]{2,1,0:T(8,128)}, f32[5,20,48]{2,1,0:T(8,128)}) custom-call(s32[16,128]{1,0:T(8,128)S(4)} %get-tuple-element.20.table_ref, f32[256,128]{1,0:T(8,128)S(1)} %bitcast.13, f32[24,16,256]{2,1,0:T(8,128)S(1)} %get-tuple-element.31.old_ref, bf16[24,208,256]{2,1,0:T(8,128)(2,1)S(1)} %get-tuple-element.29.w1_ref.w_ref), custom_call_target="tpu_custom_call" | custom-call | tf_op jit(solution)/shard_map/last/pallas_call | solution.py:584
Async XLA Ops:
  1.8 9.4 %collective-permute-start = (bf16[368,128]{1,0:T(8,128)(2,1)S(1)}, bf16[368,128]{1,0:T(8,128)(2,1)S(1)}, u32[]{:S(2)}, u32[]{:S(2)}) collective-permute-start(bf16[368,128]{1,0:T(8,128)(2,1)S(1)} %get-tuple-element.24), channel_id=1, source_target_pairs={{0,32},{32,64},{64,96},{96,128},{128,160},{160,192},{192,224},{224... | collective-permute-start | bytes 282632 | tf_op jit(solution)/shard_map/ppermute | solution.py:630
  4.4 6.9 %collective-permute-start.1 = (bf16[368,128]{1,0:T(8,128)(2,1)S(1)}, bf16[368,128]{1,0:T(8,128)(2,1)S(1)}, u32[]{:S(2)}, u32[]{:S(2)}) collective-permute-start(bf16[368,128]{1,0:T(8,128)(2,1)S(1)} %get-tuple-element.25), channel_id=1, source_target_pairs={{32,0},{64,32},{96,64},{128,96},{160,128},{192,160},{224,192},{0,2... | collective-permute-start | bytes 282632 | tf_op jit(solution)/shard_map/ppermute | solution.py:631
